TPU v7x, 256 devices: a whole 4x4x8 slice. The times are simulated.
256 devices in a mesh: dp: 4 (over y), ep: 64 (over z, x, core).
Axes of the slice: x: 4, y: 4, z: 8, core: 2. Of those that a mesh axis runs over, the one named last changes fastest.
Arguments:
- tokens: bfloat16 [24576, 2048], P(('dp', 'ep')), parts along dimension 0, may hold values from -6 to 6
- routes: int32 [24576, 8], P(('dp', 'ep')), parts along dimension 0, may hold values from 0 to 63, all different within a row; in each aligned block of 96 rows (0 to 95, 96 to 191, ...) at most 18 rows name the same one
- combine_weights: bfloat16 [24576, 8], P(('dp', 'ep')), parts along dimension 0, may hold values from 0.049804688 to 1
- w_gate: bfloat16 [64, 2048, 768], P('ep'), may hold values from -0.125 to 0.125
- w_up: bfloat16 [64, 2048, 768], P('ep'), may hold values from -0.125 to 0.125
- w_down: bfloat16 [64, 768, 2048], P('ep'), may hold values from -0.21875 to 0.21875
Outputs:
- mixed: bfloat16 [24576, 2048], P(('dp', 'ep')), parts along dimension 0
There are 4 independent parts, one for each index of `dp`. A program takes and returns all parts, laid end to end along the dimension named above; an argument that names none is the same for every part. Nothing has to cross between parts.
Inputs may be any that keep to these rules, and one draw needn't show every extreme that they name: `routes`: each row names 8 different experts. Among the 96 rows of one device no expert is named by more than 18 rows, a bound that some blocks reach.
All inputs are finite; a program needn't handle non-finite values.
Results may differ from a plain program's by a relative error of at most 0.012.
Values may be sent and summed in bfloat16 or wider, within the bound.
A program may use at most 128 MiB of HBM per device.

v0:
```python
import jax
import jax.numpy as jnp
from jax import lax
from jax.sharding import PartitionSpec as P


def expert_ffn(rows, row_weight, gate_matrix, upward_matrix, down_matrix):
    gate = jnp.dot(rows, gate_matrix, preferred_element_type=jnp.float32)
    upward = jnp.dot(rows, upward_matrix, preferred_element_type=jnp.float32)
    hidden = (jax.nn.silu(gate) * upward).astype(jnp.bfloat16)
    result = jnp.dot(hidden, down_matrix, preferred_element_type=jnp.float32)
    return (result * row_weight.astype(jnp.float32)[:, None]).astype(jnp.bfloat16)


def run_expert(arrived, arrived_weight, gate_matrix, upward_matrix, down_matrix):
    sources, slots, width = arrived.shape
    rows = arrived.reshape(sources * slots, width)
    row_weight = arrived_weight.reshape(sources * slots)
    output = expert_ffn(rows, row_weight, gate_matrix, upward_matrix, down_matrix)
    return output.reshape(sources, slots, width)


def local(tokens, routes, combine_weights, w_gate, w_up, w_down):
    peers = lax.axis_size("ep")
    local_tokens, width = tokens.shape
    top_count = routes.shape[1]
    room = min(local_tokens, 3 * local_tokens * top_count // (2 * peers))
    pair_count = local_tokens * top_count
    flat_routes = routes.reshape(-1)
    one_hot = (flat_routes[:, None] == jnp.arange(peers, dtype=jnp.int32)[None, :]).astype(
        jnp.int32
    )
    earlier = jnp.cumsum(one_hot, axis=0) - one_hot
    position = jnp.sum(earlier * one_hot, axis=1)
    slot_index = flat_routes * room + position
    owner = jnp.full((peers * room,), pair_count, jnp.int32)
    owner = owner.at[slot_index].set(jnp.arange(pair_count, dtype=jnp.int32))
    send_rows = jnp.take(tokens, owner // top_count, axis=0, mode="fill", fill_value=0)
    send_rows = send_rows.reshape(peers, room, width)
    send_weight = jnp.take(combine_weights.reshape(-1), owner, mode="fill", fill_value=0)
    send_weight = send_weight.reshape(peers, room)
    gate_matrix = w_gate[0]
    upward_matrix = w_up[0]
    down_matrix = w_down[0]
    arrived, arrived_weight = (
        lax.all_to_all(send_rows, "ep", split_axis=0, concat_axis=0, tiled=True),
        lax.all_to_all(send_weight, "ep", split_axis=0, concat_axis=0, tiled=True),
    )
    output = run_expert(arrived, arrived_weight, gate_matrix, upward_matrix, down_matrix)
    back = lax.all_to_all(output, "ep", split_axis=0, concat_axis=0, tiled=True)
    back_rows = back.reshape(peers * room, width)
    per_pair = jnp.take(back_rows, slot_index, axis=0)
    summed = jnp.sum(per_pair.reshape(local_tokens, top_count, width).astype(jnp.float32), axis=1)
    return summed.astype(jnp.bfloat16)


def solution(mesh):
    in_specs = (
        P(("dp", "ep"), None),
        P(("dp", "ep"), None),
        P(("dp", "ep"), None),
        P("ep", None, None),
        P("ep", None, None),
        P("ep", None, None),
    )
    out_specs = P(("dp", "ep"), None)
    return jax.shard_map(local, mesh=mesh, in_specs=in_specs, out_specs=out_specs, check_vma=False)
```

profile of v0, /device:TPU:1, one launch (start us, length us, event | category | flops | bytes accessed | tf_op | source)
XLA Modules:
  0.0 415.5 jit_solution(13284096876344051536)
XLA Ops:
  0.0 0.0 copy-start
  0.0 1.6 copy.19
  1.6 0.9 eq.26
  2.4 0.9 reshape.124
  3.3 0.7 broadcast_multiply_fusion
  4.0 0.7 fusion.10
  4.7 4.4 %reduce-window.6 = s32[64,6,128]{2,0,1:T(8,128)} reduce-window(s32[64,6,128]{2,0,1:T(8,128)} %fusion.10, s32[]{:T(128)} %constant.61.clone.1), window={size=1x1x128 pad=0_0x0_0x127_0}, to_apply=%region_0.0 | reduce-window | flops 6242304 | bytes 393220 | tf_op jit(solution)/shard_map/reduce-window
  9.1 1.2 slice_reduce_fusion
  10.3 0.7 copy.24
  11.0 0.9 mul.40
  11.9 1.1 fusion.9
  13.0 0.0 copy-start.4
  13.0 0.6 iota.11
  13.6 3.5 scatter_custom_fusion
  17.2 0.6 pad_clamp_fusion
  17.8 0.0 copy-done.4
  17.8 1.4 copy.25
  19.2 0.8 reshape.127
  20.0 10.3 %gather_fusion.1 = bf16[1152]{0:T(1024)(128)(2,1)} fusion(bf16[768]{0:T(1024)(128)(2,1)S(1)} %reshape.127, s32[2048]{0:T(1024)} %pad_clamp_fusion), kind=kCustom, calls=%fused_computation.1 | custom fusion | bytes 9216 | tf_op jit(solution)/shard_map/jit(_take)/gather | solution.py:40
  30.3 0.7 and_select_fusion
  31.0 0.8 select_n.65
  31.8 13.2 %all-to-all-start.1 = ((bf16[64,1,18]{2,1,0:T(2,128)(2,1)}), bf16[64,1,18]{2,1,0:T(2,128)(2,1)}, u32[]{:S(2)}, u32[]{:S(2)}) async-start(bf16[64,1,18]{2,1,0:T(2,128)(2,1)} %select_n.65), calls=%async_computation.1 | async-start | bytes 65536 | tf_op jit(solution)/shard_map/all_to_all | solution.py:47
  44.9 0.6 compare_and_fusion
  45.5 0.0 copy-done.1
  45.5 5.9 %gather_fusion = bf16[1152,2048]{1,0:T(8,128)(2,1)} fusion(bf16[96,2048]{1,0:T(8,128)(2,1)S(1)} %copy-done.1, s32[2048]{0:T(1024)S(1)} %pad_clamp_fusion.1), kind=kCustom, calls=%fused_computation | custom fusion | bytes 9441792 | tf_op jit(solution)/shard_map/jit(_take)/gather | solution.py:38
  51.5 7.6 %gather.17 = bf16[64,18,2048]{2,1,0:T(8,128)(2,1)} reshape(bf16[1152,2048]{1,0:T(8,128)(2,1)} %gather_fusion) | data formatting | bytes 9437184 | tf_op jit(solution)/shard_map/jit(_take)/gather | solution.py:38
  59.0 0.0 copy-done.6
  59.0 0.1 broadcast_in_dim.40
  59.2 6.0 %broadcast_select_fusion = bf16[64,18,2048]{2,1,0:T(8,128)(2,1)} fusion(bf16[64,18,2048]{2,1,0:T(8,128)(2,1)} %gather.17, pred[64,18]{1,0:T(8,128)(4,1)S(1)} %broadcast_in_dim.40), kind=kLoop, calls=%fused_computation.6 | loop fusion | flops 2359296 | bytes 9438336 | tf_op jit(solution)/shard_map/jit(_take)/select_n | solution.py:38
  65.1 0.0 all-to-all-done.1
  65.1 10.5 %all-to-all-start = ((bf16[64,18,2048]{2,1,0:T(8,128)(2,1)}), bf16[64,18,2048]{2,1,0:T(8,128)(2,1)}, u32[]{:S(2)}, u32[]{:S(2)}) async-start(bf16[64,18,2048]{2,1,0:T(8,128)(2,1)} %broadcast_select_fusion), calls=%async_computation | async-start | bytes 12582912 | tf_op jit(solution)/shard_map/all_to_all | solution.py:46
  75.6 0.9 convert_reduce_fusion
  76.5 0.1 reshape.130
  76.6 137.8 %all-to-all-done = bf16[64,18,2048]{2,1,0:T(8,128)(2,1)} async-done(((bf16[64,18,2048]{2,1,0:T(8,128)(2,1)}), bf16[64,18,2048]{2,1,0:T(8,128)(2,1)}, u32[]{:S(2)}, u32[]{:S(2)}) %all-to-all-start) | async-done | bytes 4718624 | tf_op jit(solution)/shard_map/all_to_all | solution.py:46
  214.4 7.8 %reshape.126 = bf16[1152,2048]{1,0:T(8,128)(2,1)} reshape(bf16[64,18,2048]{2,1,0:T(8,128)(2,1)} %all-to-all-done) | data formatting | bytes 9437184 | tf_op jit(solution)/shard_map/reshape | solution.py:17
  222.2 6.8 %fusion.5 = f32[1152,768]{1,0:T(8,128)S(1)} fusion(bf16[1152,2048]{1,0:T(8,128)(2,1)} %reshape.126, bf16[1,2048,768]{2,1,0:T(8,128)(2,1)} %param.9), kind=kOutput, calls=%fused_computation.13 | convolution fusion | flops 3623878656 | bytes 11403264 | tf_op jit(solution)/shard_map/dot_general | solution.py:8
  229.0 4.2 %fusion.1 = bf16[1152,768]{1,0:T(8,128)(2,1)S(1)} fusion(bf16[1152,2048]{1,0:T(8,128)(2,1)S(1)} %copy-done.2, f32[1152,768]{1,0:T(8,128)S(1)} %fusion.5, bf16[1,2048,768]{2,1,0:T(8,128)(2,1)S(1)} %copy-done.7), kind=kOutput, calls=%fused_computation.8 | convolution fusion | flops 3629187072 | bytes 13172736 | tf_op jit(solution)/shard_map/dot_general | solution.py:9
  233.2 0.0 copy-done
  233.2 5.5 %fusion = bf16[1152,2048]{1,0:T(8,128)(2,1)} fusion(bf16[1152,768]{1,0:T(8,128)(2,1)S(1)} %fusion.1, f32[1152]{0:T(1024)S(1)} %reshape.130, bf16[1,768,2048]{2,1,0:T(8,128)(2,1)S(1)} %copy-done), kind=kOutput, calls=%fused_computation.5 | convolution fusion | flops 3628597248 | bytes 9638400 | tf_op jit(solution)/shard_map/dot_general | solution.py:11
  238.7 7.6 %reshape.128 = bf16[64,18,2048]{2,1,0:T(8,128)(2,1)} reshape(bf16[1152,2048]{1,0:T(8,128)(2,1)} %fusion) | data formatting | bytes 9437184 | tf_op jit(solution)/shard_map/reshape | solution.py:20
  246.3 8.2 %all-to-all-start.2 = ((bf16[64,18,2048]{2,1,0:T(8,128)(2,1)}), bf16[64,18,2048]{2,1,0:T(8,128)(2,1)}, u32[]{:S(2)}, u32[]{:S(2)}) async-start(bf16[64,18,2048]{2,1,0:T(8,128)(2,1)} %reshape.128), calls=%async_computation.2 | async-start | bytes 12582912 | tf_op jit(solution)/shard_map/all_to_all | solution.py:50
  254.5 0.1 reduce_sum.26
  254.6 0.1 copy.22
  254.7 0.1 copy.23
  254.8 138.6 %all-to-all-done.2 = bf16[64,18,2048]{2,1,0:T(8,128)(2,1)} async-done(((bf16[64,18,2048]{2,1,0:T(8,128)(2,1)}), bf16[64,18,2048]{2,1,0:T(8,128)(2,1)}, u32[]{:S(2)}, u32[]{:S(2)}) %all-to-all-start.2) | async-done | bytes 4718624 | tf_op jit(solution)/shard_map/all_to_all | solution.py:50
  393.4 7.8 %reshape.129 = bf16[1152,2048]{1,0:T(8,128)(2,1)} reshape(bf16[64,18,2048]{2,1,0:T(8,128)(2,1)} %all-to-all-done.2) | data formatting | bytes 9437184 | tf_op jit(solution)/shard_map/reshape | solution.py:51
  401.2 10.0 %gather_fusion.2 = bf16[768,2048]{1,0:T(8,128)(2,1)} fusion(bf16[1152,2048]{1,0:T(8,128)(2,1)} %reshape.129, s32[1024]{0:T(1024)S(1)} %pad_clamp_fusion.2), kind=kCustom, calls=%fused_computation.2 | custom fusion | bytes 6294528 | tf_op jit(solution)/shard_map/jit(_take)/gather | solution.py:52
  411.2 4.3 %fusion.2 = bf16[96,2048]{1,0:T(8,128)(2,1)} fusion(bf16[768,2048]{1,0:T(8,128)(2,1)} %gather_fusion.2, pred[96,8]{1,0:T(8,128)(4,1)S(1)} %copy.23), kind=kLoop, calls=%fused_computation.10 | loop fusion | flops 2949120 | bytes 3539712 | tf_op jit(solution)/shard_map/reduce_sum | solution.py:53
  (16 shorter events, 0.1 us)
Async XLA Ops:
  0.0 233.2 %copy-start = (bf16[1,768,2048]{2,1,0:T(8,128)(2,1)S(1)}, bf16[1,768,2048]{2,1,0:T(8,128)(2,1)}, u32[]{:S(2)}) copy-start(bf16[1,768,2048]{2,1,0:T(8,128)(2,1)} %param.11) | copy-start | bytes 9437188
  0.0 45.5 %copy-start.1 = (bf16[96,2048]{1,0:T(8,128)(2,1)S(1)}, bf16[96,2048]{1,0:T(8,128)(2,1)}, u32[]{:S(2)}) copy-start(bf16[96,2048]{1,0:T(8,128)(2,1)} %param.6) | copy-start | bytes 1179652
  13.0 4.8 %copy-start.4 = (s32[768]{0:T(1024)}, s32[768]{0:T(1024)S(1)}, u32[]{:S(2)}) copy-start(s32[768]{0:T(1024)S(1)} %fusion.15) | copy-start | bytes 9220
  31.8 33.4 %all-to-all-start.1 = ((bf16[64,1,18]{2,1,0:T(2,128)(2,1)}), bf16[64,1,18]{2,1,0:T(2,128)(2,1)}, u32[]{:S(2)}, u32[]{:S(2)}) async-start(bf16[64,1,18]{2,1,0:T(2,128)(2,1)} %select_n.65), calls=%async_computation.1 | async-start | bytes 65536 | tf_op jit(solution)/shard_map/all_to_all | solution.py:47
  51.5 7.6 %copy-start.6 = (pred[1152]{0:T(1024)(128)(4,1)S(1)}, pred[1152]{0:T(1024)(128)(4,1)}, u32[]{:S(2)}) copy-start(pred[1152]{0:T(1024)(128)(4,1)} %get-tuple-element.5) | copy-start | bytes 3460
  65.1 149.3 %all-to-all-start = ((bf16[64,18,2048]{2,1,0:T(8,128)(2,1)}), bf16[64,18,2048]{2,1,0:T(8,128)(2,1)}, u32[]{:S(2)}, u32[]{:S(2)}) async-start(bf16[64,18,2048]{2,1,0:T(8,128)(2,1)} %broadcast_select_fusion), calls=%async_computation | async-start | bytes 12582912 | tf_op jit(solution)/shard_map/all_to_all | solution.py:46
  222.2 6.8 %copy-start.2 = (bf16[1152,2048]{1,0:T(8,128)(2,1)S(1)}, bf16[1152,2048]{1,0:T(8,128)(2,1)}, u32[]{:S(2)}) copy-start(bf16[1152,2048]{1,0:T(8,128)(2,1)} %reshape.126) | copy-start | bytes 14155780
  222.2 6.8 %copy-start.7 = (bf16[1,2048,768]{2,1,0:T(8,128)(2,1)S(1)}, bf16[1,2048,768]{2,1,0:T(8,128)(2,1)}, u32[]{:S(2)}) copy-start(bf16[1,2048,768]{2,1,0:T(8,128)(2,1)} %param.10) | copy-start | bytes 9437188
  246.3 8.4 %copy-start.3 = (s32[96,8]{0,1:T(8,128)S(1)}, s32[96,8]{0,1:T(8,128)}, u32[]{:S(2)}) copy-start(s32[96,8]{0,1:T(8,128)} %param.7) | copy-start | bytes 9220
  246.3 8.5 %copy-start.5 = (s32[768]{0:T(1024)S(1)}, s32[768]{0:T(1024)}, u32[]{:S(2)}) copy-start(s32[768]{0:T(1024)} %copy-done.4) | copy-start | bytes 9220
  246.3 147.1 %all-to-all-start.2 = ((bf16[64,18,2048]{2,1,0:T(8,128)(2,1)}), bf16[64,18,2048]{2,1,0:T(8,128)(2,1)}, u32[]{:S(2)}, u32[]{:S(2)}) async-start(bf16[64,18,2048]{2,1,0:T(8,128)(2,1)} %reshape.128), calls=%async_computation.2 | async-start | bytes 12582912 | tf_op jit(solution)/shard_map/all_to_all | solution.py:50
where the time goes:
time: 419 us; the launch traced here: 415 us
  waiting for transfers between devices  276 us (66%)
  local copies, waits for them, and re-layouts  70.8 us (17%)
  starting transfers between devices  31.9 us (8%)
  other arithmetic  19.8 us (5%)
  matrix products  16.5 us (4%)
    all_to_all x1, waiting for transfers between devices, local(): back = lax.all_to_all(output, 'ep', split_axis=0, concat_axis=0, tiled=True)  139 us
    all_to_all x1, waiting for transfers between devices, local(): lax.all_to_all(send_rows, 'ep', split_axis=0, concat_axis=0, tiled=True)  138 us
    gather x2, local copies, waits for them, and re-layouts, local(): jnp.take(tokens, owner // top_count, axis=0, mode='fill', fill_value=0)  13.5 us
    all_to_all x1, starting transfers between devices, local(): lax.all_to_all(send_weight, 'ep', split_axis=0, concat_axis=0, tiled=True)  13.2 us
    all_to_all x1, starting transfers between devices, local(): lax.all_to_all(send_rows, 'ep', split_axis=0, concat_axis=0, tiled=True)  10.5 us
    gather x1, local copies, waits for them, and re-layouts, local(): jnp.take(combine_weights.reshape(-1), owner, mode='fill', fill_value=0)  10.3 us
    gather x1, local copies, waits for them, and re-layouts, local(): per_pair = jnp.take(back_rows, slot_index, axis=0)  10 us
  transfers between devices with their start and end apart: 3, of which 2 were waited for; matrix products, arithmetic and copies ran while one was open for 5% of the time, Pallas kernels for 0%

commit v1 on v0

v1 whole, which is shorter than its diff:
```python
import jax
import jax.numpy as jnp
from jax import lax
from jax.experimental import pallas as pl
from jax.experimental.pallas import tpu as pltpu
from jax.sharding import PartitionSpec as P

MESH = pl.DeviceIdType.MESH
F32, BF16 = jnp.float32, jnp.bfloat16

NZ, NR = 8, 8
TOK, DIM, HID = 96, 2048, 768
MAIN = 16
BLK = NR * MAIN
OVF = NZ * BLK
ROWS = OVF + BLK
HALF = TOK // 2
COLS = 512

OFFSET = (0, -1, 1, -2, 2, -3, 3, 4)
STEPS = ((0, 128), (128, 256), (384, 256), (640, 256), (896, 256))


def one_hot_dot(a, b):
    return jnp.dot(a, b, preferred_element_type=F32)


def kernel(
    tokens, meta, w_gate, w_up, w_down, out,
    xz, sx, rx, ys, yr, zs, zr, wg, wu, wd, hid, pm, pmr, cm,
    local_sem, zsend, zrecv, msend, mrecv, xsend, xrecv, ysend, yrecv, rsend, rrecv,
):
    me = lax.axis_index("ep")
    z, r = me // NR, me % NR

    def at_z(d):
        return {"ep": lax.rem(z + d + NZ, NZ) * NR + r}

    def at_r(i):
        return lax.rem(r + i, NR)

    loads = [
        pltpu.make_async_copy(tokens, xz.at[0], local_sem.at[0]),
        pltpu.make_async_copy(w_gate.at[0], wg, local_sem.at[1]),
        pltpu.make_async_copy(w_up.at[0], wu, local_sem.at[2]),
        pltpu.make_async_copy(w_down.at[0], wd, local_sem.at[3]),
    ]
    for load in loads:
        load.start()

    barrier = pltpu.get_barrier_semaphore()
    for d in range(1, NZ):
        pl.semaphore_signal(barrier, inc=1, device_id=at_z(d), device_id_type=MESH)
    for i in range(1, NR):
        pl.semaphore_signal(barrier, inc=1, device_id={"ep": z * NR + at_r(i)}, device_id_type=MESH)

    expert = lax.broadcasted_iota(jnp.int32, (NZ * NR, 128), 0).astype(F32)
    named = jnp.zeros((NZ * NR, 128), F32)
    weight = jnp.zeros((NZ * NR, 128), F32)
    for k in range(8):
        hit = meta[k : k + 1, :] == expert
        named = jnp.where(hit, 1.0, named)
        weight = jnp.where(hit, meta[8 + k : 9 + k, :], weight)
    before = (
        lax.broadcasted_iota(jnp.int32, (128, 128), 0) < lax.broadcasted_iota(jnp.int32, (128, 128), 1)
    ).astype(F32).astype(BF16)
    place = one_hot_dot(named.astype(BF16), before)
    pm[:, 0:128] = jnp.where(named > 0.0, place, -1.0)
    pm[:, 128:256] = weight

    pl.semaphore_wait(barrier, NZ - 1 + NR - 1)

    def ring(k, src, dst, sem, rows=slice(0, TOK)):
        lo, n = rows.start, rows.stop - rows.start
        return pltpu.make_async_remote_copy(
            src_ref=xz.at[src, pl.ds(lo, n)], dst_ref=xz.at[dst, pl.ds(lo, n)],
            send_sem=zsend.at[sem], recv_sem=zrecv.at[sem], device_id=at_z(k), device_id_type=MESH,
        )

    loads[0].wait()
    up = [ring(1, 0, 1, 0), ring(1, 1, 3, 2), ring(1, 3, 5, 4), ring(1, 5, 7, 6, slice(0, HALF))]
    down = [ring(-1, 0, 2, 1), ring(-1, 2, 4, 3), ring(-1, 4, 6, 5), ring(-1, 6, 7, 7, slice(HALF, TOK))]
    metas = []
    for j in range(1, NZ):
        d = -OFFSET[j]
        metas.append(
            pltpu.make_async_remote_copy(
                src_ref=pm.at[pl.ds(pl.multiple_of(lax.rem(z + d + NZ, NZ) * NR, NR), NR)],
                dst_ref=pmr.at[j], send_sem=msend.at[j], recv_sem=mrecv.at[j],
                device_id=at_z(d), device_id_type=MESH,
            )
        )
    for copy in metas:
        copy.start()
    up[0].start()
    down[0].start()
    pmr[0] = pm[pl.ds(pl.multiple_of(z * NR, NR), NR), :]

    row = lax.broadcasted_iota(jnp.int32, (BLK, 128), 0)
    spread = (
        lax.broadcasted_iota(jnp.int32, (BLK, NR), 0) // MAIN == lax.broadcasted_iota(jnp.int32, (BLK, NR), 1)
    ).astype(F32).astype(BF16)

    def selections(j):
        place_j = one_hot_dot(spread, pmr[j, :, 0:128].astype(BF16))
        weight_j = one_hot_dot(spread, pmr[j, :, 128:256].astype(BF16))
        main = place_j == (row % MAIN).astype(F32)
        extra = (place_j == (MAIN + row % 2).astype(F32)) & (row % MAIN // 2 == j)
        cm[j, :, 0:BLK] = jnp.transpose(jnp.where(main, weight_j, 0.0))[0:TOK].astype(BF16)
        cm[j, :, BLK : 2 * BLK] = jnp.transpose(jnp.where(extra, weight_j, 0.0))[0:TOK].astype(BF16)
        return (
            jnp.where(main, 1.0, 0.0).astype(BF16)[:, 0:TOK],
            jnp.where(extra, 1.0, 0.0).astype(BF16)[:, 0:TOK],
        )

    mine = pl.multiple_of(r * MAIN, MAIN)

    def exchange(src, dst, first, n, send_sem, recv_sem):
        for lo in range(first, first + n, BLK):
            dst[pl.ds(lo + mine, MAIN), :] = src[pl.ds(lo + mine, MAIN), :]
        for i in range(1, NR):
            to = at_r(i)
            theirs = pl.multiple_of(to * MAIN, MAIN)
            for lo in range(first, first + n, BLK):
                pltpu.make_async_remote_copy(
                    src_ref=src.at[pl.ds(lo + theirs, MAIN)], dst_ref=dst.at[pl.ds(lo + mine, MAIN)],
                    send_sem=send_sem, recv_sem=recv_sem,
                    device_id={"ep": z * NR + to}, device_id_type=MESH,
                ).start()

    def drained(ref, n, sem):
        part = ref.at[pl.ds(0, n // BLK * (BLK - MAIN))]
        pltpu.make_async_copy(part, part, sem).wait()

    extras = []

    def gather(j):
        main, extra = selections(j)
        extras.append(extra)
        for c in range(0, DIM, COLS):
            sx[j * BLK : (j + 1) * BLK, c : c + COLS] = one_hot_dot(main, xz[j, :, c : c + COLS]).astype(BF16)

    def gather_overflow():
        for c in range(0, DIM, COLS):
            total = one_hot_dot(extras[0], xz[0, :, c : c + COLS])
            for j in range(1, NZ):
                total += one_hot_dot(extras[j], xz[j, :, c : c + COLS])
            sx[OVF:ROWS, c : c + COLS] = total.astype(BF16)

    def experts(step):
        first, n = STEPS[step]
        drained(rx, n, xrecv.at[step])

        def hidden(i, carry):
            c = pl.ds(pl.multiple_of(i * 256, 256), 256)
            rows = rx[first : first + n, :]
            gate = jnp.dot(rows, wg[:, c], preferred_element_type=F32)
            upward = jnp.dot(rows, wu[:, c], preferred_element_type=F32)
            hid[0:n, c] = (gate / (1.0 + jnp.exp(-gate)) * upward).astype(BF16)
            return carry

        def result(i, carry):
            c = pl.ds(pl.multiple_of(i * 256, 256), 256)
            ys[first : first + n, c] = jnp.dot(hid[0:n, :], wd[:, c], preferred_element_type=F32).astype(BF16)
            return carry

        lax.fori_loop(0, HID // 256, hidden, 0)
        lax.fori_loop(0, DIM // 256, result, 0)

    def dispatch(step):
        first, n = STEPS[step]
        exchange(sx, rx, first, n, xsend.at[step], xrecv.at[step])

    def give_back(step):
        first, n = STEPS[step]
        exchange(ys, yr, first, n, ysend.at[step], yrecv.at[step])

    gather(0)
    dispatch(0)
    for load in loads[1:]:
        load.wait()

    for k in (1, 2, 3):
        up[k - 1].wait_recv()
        up[k].start()
        down[k - 1].wait_recv()
        down[k].start()
        for j in (2 * k - 1, 2 * k):
            metas[j - 1].wait_recv()
            gather(j)
        dispatch(k)
        experts(k - 1)
    up[3].wait_recv()
    down[3].wait_recv()
    metas[6].wait_recv()
    gather(7)
    gather_overflow()
    dispatch(4)
    experts(3)
    give_back(3)
    experts(4)
    for step in (4, 2, 1, 0):
        give_back(step)

    def combine(j, c):
        return one_hot_dot(cm[j, :, 0:BLK], yr[j * BLK : (j + 1) * BLK, c : c + COLS]) + one_hot_dot(
            cm[j, :, BLK : 2 * BLK], yr[OVF:ROWS, c : c + COLS]
        )

    def homeward(way, m, lo, n):
        return pltpu.make_async_remote_copy(
            src_ref=zs.at[way, m, pl.ds(lo, n)], dst_ref=zr.at[way, m, pl.ds(lo, n)],
            send_sem=rsend.at[way, m], recv_sem=rrecv.at[way, m],
            device_id=at_z(1 - 2 * way), device_id_type=MESH,
        )

    spans = ((0, HALF), (HALF, HALF))
    home = [[homeward(way, 0, *spans[way])] + [homeward(way, m, 0, TOK) for m in (1, 2, 3)] for way in (0, 1)]

    drained(yr, STEPS[4][1], yrecv.at[4])
    for c in range(0, DIM, COLS):
        part = combine(7, c).astype(BF16)
        zs[0, 0, 0:HALF, c : c + COLS] = part[0:HALF]
        zs[1, 0, HALF:TOK, c : c + COLS] = part[HALF:TOK]
    for way in (0, 1):
        home[way][0].start()
    for m in (1, 2, 3):
        step = 4 - m
        drained(yr, STEPS[step][1], yrecv.at[step])
        for way, j in ((0, 2 * step), (1, 2 * step - 1)):
            home[way][m - 1].wait_recv()
            for c in range(0, DIM, COLS):
                part = combine(j, c)
                if m == 1:
                    lo, n = spans[way]
                    came = zr[way, 0, lo : lo + n, c : c + COLS].astype(F32)
                    zs[way, 1, lo : lo + n, c : c + COLS] = (part[lo : lo + n] + came).astype(BF16)
                    lo = HALF - lo
                    zs[way, 1, lo : lo + n, c : c + COLS] = part[lo : lo + n].astype(BF16)
                else:
                    came = zr[way, m - 1, :, c : c + COLS].astype(F32)
                    zs[way, m, :, c : c + COLS] = (part + came).astype(BF16)
            home[way][m].start()
    drained(yr, STEPS[0][1], yrecv.at[0])
    home[0][3].wait_recv()
    home[1][3].wait_recv()
    for c in range(0, DIM, COLS):
        total = combine(0, c) + zr[0, 3, :, c : c + COLS].astype(F32) + zr[1, 3, :, c : c + COLS].astype(F32)
        out[:, c : c + COLS] = total.astype(BF16)

    for copy in up + down + metas + home[0] + home[1]:
        copy.wait_send()
    for step in range(5):
        drained(sx, STEPS[step][1], xsend.at[step])
        drained(ys, STEPS[step][1], ysend.at[step])


def local(tokens, routes, combine_weights, w_gate, w_up, w_down):
    meta = jnp.concatenate([routes.T.astype(F32), combine_weights.T.astype(F32)], axis=0)
    meta = jnp.pad(meta, ((0, 0), (0, 128 - TOK)), constant_values=-1.0)
    anywhere = pl.BlockSpec(memory_space=pl.ANY)
    vmem = pl.BlockSpec(memory_space=pltpu.VMEM)
    dma = pltpu.SemaphoreType.DMA
    return pl.pallas_call(
        kernel,
        name="routed_experts",
        out_shape=jax.ShapeDtypeStruct((TOK, DIM), BF16),
        in_specs=[anywhere, vmem, anywhere, anywhere, anywhere],
        out_specs=vmem,
        scratch_shapes=[
            pltpu.VMEM((NZ, TOK, DIM), BF16),
            pltpu.VMEM((ROWS, DIM), BF16),
            pltpu.VMEM((ROWS, DIM), BF16),
            pltpu.VMEM((ROWS, DIM), BF16),
            pltpu.VMEM((ROWS, DIM), BF16),
            pltpu.VMEM((2, 4, TOK, DIM), BF16),
            pltpu.VMEM((2, 4, TOK, DIM), BF16),
            pltpu.VMEM((DIM, HID), BF16),
            pltpu.VMEM((DIM, HID), BF16),
            pltpu.VMEM((HID, DIM), BF16),
            pltpu.VMEM((256, HID), BF16),
            pltpu.VMEM((NZ * NR, 256), F32),
            pltpu.VMEM((NZ, NR, 256), F32),
            pltpu.VMEM((NZ, TOK, 2 * BLK), BF16),
            dma((4,)), dma((8,)), dma((8,)), dma((8,)), dma((8,)),
            dma((5,)), dma((5,)), dma((5,)), dma((5,)), dma((2, 4)), dma((2, 4)),
        ],
        compiler_params=pltpu.CompilerParams(
            collective_id=0, has_side_effects=True, vmem_limit_bytes=67_043_328
        ),
    )(tokens, meta, w_gate, w_up, w_down)


def solution(mesh):
    in_specs = (
        P(("dp", "ep"), None), P(("dp", "ep"), None), P(("dp", "ep"), None),
        P("ep", None, None), P("ep", None, None), P("ep", None, None),
    )
    return jax.shard_map(
        local, mesh=mesh, in_specs=in_specs, out_specs=P(("dp", "ep"), None), check_vma=False
    )
```

time: 419 us -> 134 us (0.32)
  waiting for transfers between devices: 276 us -> 0 us
  Pallas kernels: 0 us -> 130 us
  local copies, waits for them, and re-layouts: 70.8 us -> 1.77 us
  starting transfers between devices: 31.9 us -> 0 us
  other arithmetic: 19.8 us -> 1.98 us
  matrix products: 16.5 us -> 0 us
    all_to_all x3 -> x0, waiting for transfers between devices: 276 us -> none  [the longest x1 139 us: local(): back = lax.all_to_all(output, 'ep', split_axis=0, concat_axis=0, tiled=True)]
    pallas_call x0 -> x1, Pallas kernels: none -> 130 us  [local(): pl.pallas_call(kernel, name='routed_experts', out_shape=jax.ShapeDtypeStr...]
    gather x4 -> x0, local copies, waits for them, and re-layouts: 33.8 us -> none  [the longest x2 13.5 us: local(): jnp.take(tokens, owner // top_count, axis=0, mode='fill', fill_value=0)]
    all_to_all x3 -> x0, starting transfers between devices: 31.9 us -> none  [the longest x1 13.2 us: local(): lax.all_to_all(send_weight, 'ep', split_axis=0, concat_axis=0, tiled=True)]
    reshape x5 -> x0, local copies, waits for them, and re-layouts: 24.8 us -> none  [the longest x1 7.77 us: run_expert(): rows = arrived.reshape(sources * slots, width)]
    dot_general x3 -> x0, matrix products: 16.5 us -> none  [the longest x1 6.76 us: expert_ffn(): gate = jnp.dot(rows, gate_matrix, preferred_element_type=jnp.float32)]
    select_n x4 -> x0, other arithmetic: 6.67 us -> none  [the longest x1 5.95 us: local(): jnp.take(tokens, owner // top_count, axis=0, mode='fill', fill_value=0)]
    reduce_sum x2 -> x0, other arithmetic: 5.32 us -> none  [the longest x1 4.26 us: local(): jnp.sum(per_pair.reshape(local_tokens, top_count, width).astype(jnp.float...]
  transfers between devices with their start and end apart: 3 -> 0, of which waited for: 2 -> 0; matrix products, arithmetic and copies ran while one was open for 5% -> 0% of each run, Pallas kernels for 0% -> 0%
where the time goes in v1:
time: 134 us
  Pallas kernels  130 us (97%)
  other arithmetic  1.98 us (1%)
  local copies, waits for them, and re-layouts  1.77 us (1%)
    pallas_call x1, Pallas kernels, local(): pl.pallas_call(kernel, name='routed_experts', out_shape=jax.ShapeDtypeStr...  130 us

profile of v1, /device:TPU:1, one launch (start us, length us, event | category | flops | bytes accessed | tf_op | source)
XLA Modules:
  0.0 134.1 jit_solution(7219793199820027084)
XLA Ops:
  0.0 0.7 convert_bitcast_fusion.1
  0.7 0.7 convert_bitcast_fusion
  1.4 0.6 select_maximum_fusion.meta
  2.0 130.3 %routed_experts.1 = bf16[96,2048]{1,0:T(8,128)(2,1)} custom-call(bf16[96,2048]{1,0:T(8,128)(2,1)} %tokens.1, f32[16,128]{1,0:T(8,128)} %select_maximum_fusion.meta, bf16[1,2048,768]{2,1,0:T(8,128)(2,1)} %w_gate.1, bf16[1,2048,768]{2,1,0:T(8,128)(2,1)} %w_up.1, bf16[1,768,2048]{2,1,0:T(8,128)(2,1)} %w_down.1), custom_call_target="tpu_custom_call" | custom-call | tf_op jit(solution)/shard_map/routed_experts/pallas_call | solution.py:264
  132.3 1.8 %copy.8 = bf16[96,2048]{1,0:T(8,128)(2,1)} copy(bf16[96,2048]{1,0:T(8,128)(2,1)} %routed_experts.1) | data formatting | bytes 786432

commit v2 on v1

v2 whole, which is shorter than its diff:
```python
import jax
import jax.numpy as jnp
from jax import lax
from jax.experimental import pallas as pl
from jax.experimental.pallas import tpu as pltpu
from jax.sharding import PartitionSpec as P

MESH = pl.DeviceIdType.MESH
F32, BF16 = jnp.float32, jnp.bfloat16

NZ, NR = 8, 8
TOK, DIM, HID = 96, 2048, 768
MAIN = 16
BLK = NR * MAIN
OVF = NZ * BLK
ROWS = OVF + BLK
HALF = TOK // 2
PARTS = 4
COLS = DIM // PARTS

OFFSET = (0, -1, 1, -2, 2, -3, 3, 4)
STEPS = ((0, 128), (128, 256), (384, 256), (640, 256), (896, 256))


def one_hot_dot(a, b):
    return jnp.dot(a, b, preferred_element_type=F32)


def kernel(
    tokens, routes, weights, w_gate, w_up, w_down, out,
    xz, sx, rx, ys, yr, zs, zr, wg, wu, wd, hid, square, meta, cm,
    local_sem, zsend, zrecv, msend, mrecv, xsend, xrecv, ysend, yrecv, rsend, rrecv,
):
    me = lax.axis_index("ep")
    z, r = me // NR, me % NR

    def at_z(d):
        return {"ep": lax.rem(z + d + NZ, NZ) * NR + r}

    def at_r(i):
        return lax.rem(r + i, NR)

    loads = [
        pltpu.make_async_copy(tokens, xz.at[0], local_sem.at[0]),
        pltpu.make_async_copy(w_gate.at[0], wg, local_sem.at[1]),
        pltpu.make_async_copy(w_up.at[0], wu, local_sem.at[2]),
        pltpu.make_async_copy(w_down.at[0], wd, local_sem.at[3]),
    ]
    for load in loads:
        load.start()

    barrier = pltpu.get_barrier_semaphore()
    for d in (-1, 1):
        pl.semaphore_signal(barrier, inc=1, device_id=at_z(d), device_id_type=MESH)
    for i in range(1, NR):
        pl.semaphore_signal(barrier, inc=1, device_id={"ep": z * NR + at_r(i)}, device_id_type=MESH)

    square[...] = jnp.full((128, 128), -1.0, F32)
    square[0:TOK, 0:8] = routes[...].astype(F32)
    square[0:TOK, 8:16] = weights[...].astype(F32)
    meta[0] = jnp.transpose(square[...])[0:16]

    pl.semaphore_wait(barrier, 2 + NR - 1)

    def ring(k, src, dst, sem, rows=slice(0, TOK)):
        lo, n = rows.start, rows.stop - rows.start
        return [
            pltpu.make_async_remote_copy(
                src_ref=xz.at[src, pl.ds(lo, n), pl.ds(h * COLS, COLS)],
                dst_ref=xz.at[dst, pl.ds(lo, n), pl.ds(h * COLS, COLS)],
                send_sem=zsend.at[sem, h], recv_sem=zrecv.at[sem, h], device_id=at_z(k), device_id_type=MESH,
            )
            for h in range(PARTS)
        ]

    def table(k, src, dst):
        return pltpu.make_async_remote_copy(
            src_ref=meta.at[src], dst_ref=meta.at[dst], send_sem=msend.at[dst], recv_sem=mrecv.at[dst],
            device_id=at_z(k), device_id_type=MESH,
        )

    up = [ring(1, 0, 1, 0), ring(1, 1, 3, 2), ring(1, 3, 5, 4), ring(1, 5, 7, 6, slice(0, HALF))]
    down = [ring(-1, 0, 2, 1), ring(-1, 2, 4, 3), ring(-1, 4, 6, 5), ring(-1, 6, 7, 7, slice(HALF, TOK))]
    metas = [None, table(1, 0, 1), table(-1, 0, 2), table(1, 1, 3), table(-1, 2, 4), table(1, 3, 5), table(-1, 4, 6), table(1, 5, 7)]
    metas[1].start()
    metas[2].start()
    loads[0].wait()
    for h in range(PARTS):
        up[0][h].start()
        down[0][h].start()

    row = lax.broadcasted_iota(jnp.int32, (BLK, 128), 0)
    spread = (
        lax.broadcasted_iota(jnp.int32, (BLK, NR), 0) // MAIN == lax.broadcasted_iota(jnp.int32, (BLK, NR), 1)
    ).astype(F32).astype(BF16)

    before = (
        lax.broadcasted_iota(jnp.int32, (128, 128), 0) < lax.broadcasted_iota(jnp.int32, (128, 128), 1)
    ).astype(F32).astype(BF16)
    expert = (lax.broadcasted_iota(jnp.int32, (NR, 128), 0) + z * NR).astype(F32)

    def selections(j):
        named = jnp.zeros((NR, 128), F32)
        weight = jnp.zeros((NR, 128), F32)
        for k in range(8):
            hit = meta[j, k : k + 1, :] == expert
            named = jnp.where(hit, 1.0, named)
            weight = jnp.where(hit, meta[j, 8 + k : 9 + k, :], weight)
        place = jnp.where(named > 0.0, one_hot_dot(named.astype(BF16), before), -1.0)
        place_j = one_hot_dot(spread, place.astype(BF16))
        weight_j = one_hot_dot(spread, weight.astype(BF16))
        main = place_j == (row % MAIN).astype(F32)
        extra = (place_j == (MAIN + row % 2).astype(F32)) & (row % MAIN // 2 == j)
        cm[j, :, 0:BLK] = jnp.transpose(jnp.where(main, weight_j, 0.0))[0:TOK].astype(BF16)
        cm[j, :, BLK : 2 * BLK] = jnp.transpose(jnp.where(extra, weight_j, 0.0))[0:TOK].astype(BF16)
        return (
            jnp.where(main, 1.0, 0.0).astype(BF16)[:, 0:TOK],
            jnp.where(extra, 1.0, 0.0).astype(BF16)[:, 0:TOK],
        )

    mine = pl.multiple_of(r * MAIN, MAIN)

    def exchange(src, dst, first, n, send_sem, recv_sem, c, w):
        for lo in range(first, first + n, BLK):
            dst[pl.ds(lo + mine, MAIN), c : c + w] = src[pl.ds(lo + mine, MAIN), c : c + w]
        for i in range(1, NR):
            to = at_r(i)
            theirs = pl.multiple_of(to * MAIN, MAIN)
            for lo in range(first, first + n, BLK):
                pltpu.make_async_remote_copy(
                    src_ref=src.at[pl.ds(lo + theirs, MAIN), pl.ds(c, w)],
                    dst_ref=dst.at[pl.ds(lo + mine, MAIN), pl.ds(c, w)],
                    send_sem=send_sem, recv_sem=recv_sem,
                    device_id={"ep": z * NR + to}, device_id_type=MESH,
                ).start()

    def drained(ref, n, sem, w=DIM):
        part = ref.at[pl.ds(0, n // BLK * (BLK - MAIN)), pl.ds(0, w)]
        pltpu.make_async_copy(part, part, sem).wait()

    extras = []

    picks = {}

    def gather(j, h):
        if h == 0:
            picks[j], extra = selections(j)
            extras.append(extra)
        c = h * COLS
        sx[j * BLK : (j + 1) * BLK, c : c + COLS] = one_hot_dot(picks[j], xz[j, :, c : c + COLS]).astype(BF16)

    def gather_overflow():
        for c in range(0, DIM, COLS):
            total = one_hot_dot(extras[0], xz[0, :, c : c + COLS])
            for j in range(1, NZ):
                total += one_hot_dot(extras[j], xz[j, :, c : c + COLS])
            sx[OVF:ROWS, c : c + COLS] = total.astype(BF16)

    def experts(step):
        first, n = STEPS[step]
        drained(rx, n, xrecv.at[step])

        def hidden(i, carry):
            c = pl.ds(pl.multiple_of(i * 256, 256), 256)
            rows = rx[first : first + n, :]
            gate = jnp.dot(rows, wg[:, c], preferred_element_type=F32)
            upward = jnp.dot(rows, wu[:, c], preferred_element_type=F32)
            hid[0:n, c] = (gate / (1.0 + jnp.exp(-gate)) * upward).astype(BF16)
            return carry

        def result(i, carry):
            c = pl.ds(pl.multiple_of(i * 256, 256), 256)
            ys[first : first + n, c] = jnp.dot(hid[0:n, :], wd[:, c], preferred_element_type=F32).astype(BF16)
            return carry

        lax.fori_loop(0, HID // 256, hidden, 0)
        lax.fori_loop(0, DIM // 256, result, 0)

    def dispatch(step, c=0, w=DIM):
        first, n = STEPS[step]
        exchange(sx, rx, first, n, xsend.at[step], xrecv.at[step], c, w)

    def give_back(step):
        first, n = STEPS[step]
        for h in range(PARTS):
            exchange(ys, yr, first, n, ysend.at[step], yrecv.at[step, h], h * COLS, COLS)

    def arrive(k):
        for j in (2 * k - 1, 2 * k):
            metas[j].wait_recv()
            if j + 2 < NZ:
                metas[j + 2].start()
        for h in range(PARTS):
            up[k - 1][h].wait_recv()
            up[k][h].start()
            down[k - 1][h].wait_recv()
            down[k][h].start()
            gather(2 * k - 1, h)
            gather(2 * k, h)
            if k == 1:
                dispatch(1, h * COLS, COLS)
        if k > 1:
            dispatch(k)

    for h in range(PARTS):
        gather(0, h)
        dispatch(0, h * COLS, COLS)
    for load in loads[1:]:
        load.wait()
    arrive(1)
    experts(0)
    arrive(2)
    experts(1)
    arrive(3)
    metas[7].wait_recv()
    for h in range(PARTS):
        up[3][h].wait_recv()
        down[3][h].wait_recv()
        gather(7, h)
    gather_overflow()
    dispatch(4)
    experts(2)
    experts(3)
    give_back(3)
    experts(4)
    for step in (4, 2, 1, 0):
        give_back(step)

    def combine(j, c):
        return one_hot_dot(cm[j, :, 0:BLK], yr[j * BLK : (j + 1) * BLK, c : c + COLS]) + one_hot_dot(
            cm[j, :, BLK : 2 * BLK], yr[OVF:ROWS, c : c + COLS]
        )

    def homeward(way, m, lo, n):
        return [
            pltpu.make_async_remote_copy(
                src_ref=zs.at[way, m, pl.ds(lo, n), pl.ds(h * COLS, COLS)],
                dst_ref=zr.at[way, m, pl.ds(lo, n), pl.ds(h * COLS, COLS)],
                send_sem=rsend.at[way, m, h], recv_sem=rrecv.at[way, m, h],
                device_id=at_z(1 - 2 * way), device_id_type=MESH,
            )
            for h in range(PARTS)
        ]

    spans = ((0, HALF), (HALF, HALF))
    home = [[homeward(way, 0, *spans[way])] + [homeward(way, m, 0, TOK) for m in (1, 2, 3)] for way in (0, 1)]

    for h in range(PARTS):
        c = h * COLS
        drained(yr, STEPS[4][1], yrecv.at[4, h], COLS)
        part = combine(7, c).astype(BF16)
        for way in (0, 1):
            lo, n = spans[way]
            zs[way, 0, lo : lo + n, c : c + COLS] = part[lo : lo + n]
            home[way][0][h].start()
    for m in (1, 2, 3):
        step = 4 - m
        for h in range(PARTS):
            c = h * COLS
            drained(yr, STEPS[step][1], yrecv.at[step, h], COLS)
            for way, j in ((0, 2 * step), (1, 2 * step - 1)):
                part = combine(j, c)
                home[way][m - 1][h].wait_recv()
                if m == 1:
                    lo, n = spans[way]
                    came = zr[way, 0, lo : lo + n, c : c + COLS].astype(F32)
                    zs[way, 1, lo : lo + n, c : c + COLS] = (part[lo : lo + n] + came).astype(BF16)
                    lo = HALF - lo
                    zs[way, 1, lo : lo + n, c : c + COLS] = part[lo : lo + n].astype(BF16)
                else:
                    came = zr[way, m - 1, :, c : c + COLS].astype(F32)
                    zs[way, m, :, c : c + COLS] = (part + came).astype(BF16)
                home[way][m][h].start()
    for h in range(PARTS):
        c = h * COLS
        drained(yr, STEPS[0][1], yrecv.at[0, h], COLS)
        part = combine(0, c)
        home[0][3][h].wait_recv()
        home[1][3][h].wait_recv()
        total = part + zr[0, 3, :, c : c + COLS].astype(F32) + zr[1, 3, :, c : c + COLS].astype(F32)
        out[:, c : c + COLS] = total.astype(BF16)

    for message in up + down + home[0] + home[1]:
        for copy in message:
            copy.wait_send()
    for copy in metas[1:]:
        copy.wait_send()
    for step in range(5):
        drained(sx, STEPS[step][1], xsend.at[step])
        drained(ys, STEPS[step][1], ysend.at[step])


def local(tokens, routes, combine_weights, w_gate, w_up, w_down):
    anywhere = pl.BlockSpec(memory_space=pl.ANY)
    vmem = pl.BlockSpec(memory_space=pltpu.VMEM)
    dma = pltpu.SemaphoreType.DMA
    return pl.pallas_call(
        kernel,
        name="routed_experts",
        out_shape=jax.ShapeDtypeStruct((TOK, DIM), BF16),
        in_specs=[anywhere, vmem, vmem, anywhere, anywhere, anywhere],
        out_specs=vmem,
        scratch_shapes=[
            pltpu.VMEM((NZ, TOK, DIM), BF16),
            pltpu.VMEM((ROWS, DIM), BF16),
            pltpu.VMEM((ROWS, DIM), BF16),
            pltpu.VMEM((ROWS, DIM), BF16),
            pltpu.VMEM((ROWS, DIM), BF16),
            pltpu.VMEM((2, 4, TOK, DIM), BF16),
            pltpu.VMEM((2, 4, TOK, DIM), BF16),
            pltpu.VMEM((DIM, HID), BF16),
            pltpu.VMEM((DIM, HID), BF16),
            pltpu.VMEM((HID, DIM), BF16),
            pltpu.VMEM((256, HID), BF16),
            pltpu.VMEM((128, 128), F32),
            pltpu.VMEM((NZ, 16, 128), F32),
            pltpu.VMEM((NZ, TOK, 2 * BLK), BF16),
            dma((4,)), dma((8, PARTS)), dma((8, PARTS)), dma((8,)), dma((8,)),
            dma((5,)), dma((5,)), dma((5,)), dma((5, PARTS)), dma((2, 4, PARTS)), dma((2, 4, PARTS)),
        ],
        compiler_params=pltpu.CompilerParams(
            collective_id=0, has_side_effects=True, vmem_limit_bytes=67_043_328
        ),
    )(tokens, routes, combine_weights, w_gate, w_up, w_down)


def solution(mesh):
    in_specs = (
        P(("dp", "ep"), None), P(("dp", "ep"), None), P(("dp", "ep"), None),
        P("ep", None, None), P("ep", None, None), P("ep", None, None),
    )
    return jax.shard_map(
        local, mesh=mesh, in_specs=in_specs, out_specs=P(("dp", "ep"), None), check_vma=False
    )
```

time: 134 us -> 124 us (0.925)
  Pallas kernels: 130 us -> 119 us
  local copies, waits for them, and re-layouts: 1.77 us -> 4.54 us
  other arithmetic: 1.98 us -> 0 us
    pallas_call x1, Pallas kernels: 130 us -> 119 us  [local(): pl.pallas_call(kernel, name='routed_experts', out_shape=jax.ShapeDtypeStr...]
    unnamed x1 -> x3, local copies, waits for them, and re-layouts: 1.77 us -> 4.54 us
    convert_element_type x2 -> x0, other arithmetic: 1.37 us -> none  [the longest x1 0.69 us: local(): routes.T.astype(F32)]
where the time goes in v2:
time: 124 us
  Pallas kernels  119 us (96%)
  local copies, waits for them, and re-layouts  4.54 us (4%)
    pallas_call x1, Pallas kernels, local(): pl.pallas_call(kernel, name='routed_experts', out_shape=jax.ShapeDtypeStr...  119 us
    unnamed x3, local copies, waits for them, and re-layouts  4.54 us

profile of v2, /device:TPU:1, one launch (start us, length us, event | category | flops | bytes accessed | tf_op | source)
XLA Modules:
  0.0 123.8 jit_solution(11818156166503976297)
XLA Ops:
  0.0 1.4 %copy.8.weights = bf16[96,8]{1,0:T(8,128)(2,1)} copy(bf16[96,8]{0,1:T(8,128)(2,1)} %param.8) | data formatting | bytes 3072 | tf_op args[2]
  1.4 1.4 %copy.7.routes = s32[96,8]{1,0:T(8,128)} copy(s32[96,8]{0,1:T(8,128)} %param.7) | data formatting | bytes 6144 | tf_op args[1]
  2.8 119.3 %routed_experts.1 = bf16[96,2048]{1,0:T(8,128)(2,1)} custom-call(bf16[96,2048]{1,0:T(8,128)(2,1)} %tokens.1, s32[96,8]{1,0:T(8,128)} %copy.7.routes, bf16[96,8]{1,0:T(8,128)(2,1)} %copy.8.weights, bf16[1,2048,768]{2,1,0:T(8,128)(2,1)} %w_gate.1, bf16[1,2048,768]{2,1,0:T(8,128)(2,1)} %w_up.1, bf16[1,768,2048]{2,1,0:T(8,128)(2,1)} %w_down.1), custom_call_target="tpu_custom_call" | custom-call | tf_op jit(solution)/shard_map/routed_experts/pallas_call | solution.py:297
  122.0 1.8 %copy.10 = bf16[96,2048]{1,0:T(8,128)(2,1)} copy(bf16[96,2048]{1,0:T(8,128)(2,1)} %routed_experts.1) | data formatting | bytes 786432

commit v3 on v2

v3 whole, which is shorter than its diff:
```python
import jax
import jax.numpy as jnp
from jax import lax
from jax.experimental import pallas as pl
from jax.experimental.pallas import tpu as pltpu
from jax.sharding import PartitionSpec as P

MESH = pl.DeviceIdType.MESH
F32, BF16 = jnp.float32, jnp.bfloat16

NZ, NX, NR = 8, 4, 8
TOK, DIM, HID = 96, 2048, 768
MAIN = 16
BLK = NR * MAIN
OVF = NZ * BLK
ROWS = OVF + BLK
HALF = TOK // 2
NEAR = 4 * MAIN

PARTS, DUAL = 4, 1
FULL = PARTS - DUAL
COLS = DIM // PARTS
DCOLS = DUAL * COLS
WIDE = DIM + DCOLS
SECOND = tuple(range(PARTS, PARTS + DUAL))
RETURNED = tuple(range(FULL, PARTS)) + tuple(range(FULL))

OFFSET = (0, -1, 1, -2, 2, -3, 3, 4)
SLOTS = ((0,), (1, 2), (3, 4), (5, 6), (7,))


def dot(a, b):
    return jnp.dot(a, b, preferred_element_type=F32)


def iota(shape, axis):
    return lax.broadcasted_iota(jnp.int32, shape, axis)


def kernel(
    tokens, routes, weights, w_gate, w_up, w_down, out,
    xz, sx, rx, ys, yr, so, sn, yo, yn, zs, zr, fs, fr,
    wg, wu, wd, hid, listed, weighed, square, meta, metn, cm, co, cn,
    local_sem, zsend, zrecv, msend, mrecv, nsend, nrecv, dsend, drecv,
    xsend, xrecv, tsend, trecv, osend, orecv, ysend, yrecv, psend, precv, rsend, rrecv, fsend, frecv,
):
    me = lax.axis_index("ep")
    z, r = me // NR, me % NR
    x, c = r // 2, r % 2
    s = 1 - 2 * c

    def at_z(d):
        return {"ep": lax.rem(z + d + NZ, NZ) * NR + r}

    def in_row(other):
        return {"ep": z * NR + other}

    def device(dx, core):
        return lax.rem(x + dx + 2 * NX, NX) * 2 + core

    def tile(row):
        return pl.ds(pl.multiple_of(row, MAIN), MAIN)

    second, host_of = device(s, c), device(-s, c)
    loads = [
        pltpu.make_async_copy(routes, listed, local_sem.at[0]),
        pltpu.make_async_copy(weights, weighed, local_sem.at[1]),
        pltpu.make_async_copy(tokens, xz.at[0, :, pl.ds(0, DIM)], local_sem.at[2]),
        pltpu.make_async_copy(w_gate.at[0], wg, local_sem.at[3]),
        pltpu.make_async_copy(w_up.at[0], wu, local_sem.at[4]),
        pltpu.make_async_copy(w_down.at[0], wd, local_sem.at[5]),
    ]
    barrier = pltpu.get_barrier_semaphore()
    for d in (-1, 1):
        pl.semaphore_signal(barrier, inc=1, device_id=at_z(d), device_id_type=MESH)
    for i in range(1, NR):
        pl.semaphore_signal(barrier, inc=1, device_id=in_row(lax.rem(r + i, NR)), device_id_type=MESH)
    for load in loads:
        load.start()

    square[...] = jnp.full((128, 128), -1.0, F32)
    loads[0].wait()
    square[0:TOK, 0:8] = listed[...].astype(F32)
    loads[1].wait()
    square[0:TOK, 8:16] = weighed[...].astype(F32)
    meta[0] = jnp.transpose(square[...])[0:16]

    def ring(k, src, dst, sem, lo=0, n=TOK):
        return [
            pltpu.make_async_remote_copy(
                src_ref=xz.at[src, pl.ds(lo, n), pl.ds(h * COLS, COLS)],
                dst_ref=xz.at[dst, pl.ds(lo, n), pl.ds(h * COLS, COLS)],
                send_sem=zsend.at[sem, h], recv_sem=zrecv.at[sem, h], device_id=at_z(k), device_id_type=MESH,
            )
            for h in range(PARTS + DUAL)
        ]

    def tables(ref, send, recv):
        return [None] + [
            pltpu.make_async_remote_copy(
                src_ref=ref.at[max(j - 2, 0)], dst_ref=ref.at[j], send_sem=send.at[j], recv_sem=recv.at[j],
                device_id=at_z(1 if j % 2 else -1), device_id_type=MESH,
            )
            for j in range(1, NZ)
        ]

    up = [ring(1, 0, 1, 0), ring(1, 1, 3, 2), ring(1, 3, 5, 4), ring(1, 5, 7, 6, 0, HALF)]
    down = [ring(-1, 0, 2, 1), ring(-1, 2, 4, 3), ring(-1, 4, 6, 5), ring(-1, 6, 7, 7, HALF, HALF)]
    metas, metns = tables(meta, msend, mrecv), tables(metn, nsend, nrecv)
    dense = [
        pltpu.make_async_remote_copy(
            src_ref=xz.at[0, :, pl.ds((FULL + i) * COLS, COLS)], dst_ref=xz.at[0, :, pl.ds((PARTS + i) * COLS, COLS)],
            send_sem=dsend.at[i], recv_sem=drecv.at[i], device_id=in_row(second), device_id_type=MESH,
        )
        for i in range(DUAL)
    ]
    dense_table = pltpu.make_async_remote_copy(
        src_ref=meta.at[0], dst_ref=metn.at[0], send_sem=nsend.at[0], recv_sem=nrecv.at[0],
        device_id=in_row(second), device_id_type=MESH,
    )

    pl.semaphore_wait(barrier, 2 + NR - 1)
    metas[1].start()
    metas[2].start()
    dense_table.start()
    loads[2].wait()
    for h in range(PARTS):
        up[0][h].start()
        down[0][h].start()
    for copy in dense:
        copy.start()

    before = (iota((128, 128), 0) < iota((128, 128), 1)).astype(F32).astype(BF16)
    expert = (iota((NR, 128), 0) + z * NR).astype(F32)
    row = iota((BLK, 128), 0)
    near = row[0:NEAR]

    def spread(of, rows):
        return (of == iota((rows, NR), 1)).astype(F32).astype(BF16)

    served = iota((NEAR, NR), 0) // MAIN
    all_rows = spread(iota((BLK, NR), 0) // MAIN, BLK)
    own_rows = spread(jnp.where(served < 2, 2 * x + served, device(-s, 0) + served - 2), NEAR)
    second_rows = spread(jnp.where(served < 2, 2 * x + served, device(s, 0) + served - 2), NEAR)

    def lists(ref, j):
        named = jnp.zeros((NR, 128), F32)
        weight = jnp.zeros((NR, 128), F32)
        for k in range(8):
            hit = ref[j, k : k + 1, :] == expert
            named = jnp.where(hit, 1.0, named)
            weight = jnp.where(hit, ref[j, 8 + k : 9 + k, :], weight)
        place = jnp.where(named > 0.0, dot(named.astype(BF16), before), -1.0)
        return place.astype(BF16), weight.astype(BF16)

    def pick(mask, weight, ref, j, lo, n):
        ref[j, :, lo : lo + n] = jnp.transpose(jnp.where(mask, weight, 0.0))[0:TOK].astype(BF16)
        return jnp.where(mask, 1.0, 0.0).astype(BF16)[:, 0:TOK]

    picks, extras, own_picks, second_picks = {}, {}, {}, {}

    def selections(j):
        place, weight = lists(meta, j)
        place_j, weight_j = dot(all_rows, place), dot(all_rows, weight)
        picks[j] = pick(place_j == (row % MAIN).astype(F32), weight_j, cm, j, 0, BLK)
        extra = (place_j == (MAIN + row % 2).astype(F32)) & (row % MAIN // 2 == j)
        extras[j] = pick(extra, weight_j, cm, j, BLK, BLK)
        own_picks[j] = pick(dot(own_rows, place) == (near % MAIN).astype(F32), dot(own_rows, weight), co, j, 0, NEAR)

    def second_selections(j):
        place, weight = lists(metn, j)
        second_picks[j] = pick(
            dot(second_rows, place) == (near % MAIN).astype(F32), dot(second_rows, weight), cn, j, 0, NEAR
        )

    mine, hosted = r * MAIN, host_of * MAIN

    def send(src, dst, send_sem, recv_sem, to):
        pltpu.make_async_remote_copy(
            src_ref=src, dst_ref=dst, send_sem=send_sem, recv_sem=recv_sem, device_id=in_row(to), device_id_type=MESH
        ).start()

    def exchange(src, dst, lo, send_sem, recv_sem, col, w):
        cols = pl.ds(col, w)
        dst[tile(lo + mine), cols] = src[tile(lo + mine), cols]
        for i in range(1, NR):
            to = lax.rem(r + i, NR)
            send(src.at[tile(lo + to * MAIN), cols], dst.at[tile(lo + mine), cols], send_sem, recv_sem, to)

    def settle(rows, w, sem):
        part = rx.at[pl.ds(0, rows), pl.ds(0, w)]
        pltpu.make_async_copy(part, part, sem).wait()

    def gather(step, h, slots=None):
        for j in slots or SLOTS[step]:
            if j not in picks:
                selections(j)
            if h < FULL:
                sx[j * BLK : (j + 1) * BLK, h * COLS : (h + 1) * COLS] = dot(
                    picks[j], xz[j, :, h * COLS : (h + 1) * COLS]
                ).astype(BF16)
                exchange(sx, rx, j * BLK, xsend.at[step], xrecv.at[step], h * COLS, COLS)
            elif h < PARTS:
                serve(step, j, h, h - FULL, own_picks[j], so, mine, 0 - s)
            else:
                if h == PARTS:
                    second_selections(j)
                serve(step, j, h, h - PARTS, second_picks[j], sn, hosted, s)

    def serve(step, j, h, i, picked, src, home, far):
        cols, to_cols = pl.ds(i * COLS, COLS), pl.ds((FULL + i) * COLS, COLS)
        src[j * NEAR : (j + 1) * NEAR, cols] = dot(picked, xz[j, :, h * COLS : (h + 1) * COLS]).astype(BF16)
        dst = tile(j * BLK + home)
        rx[dst, to_cols] = src[tile(j * NEAR + c * MAIN), cols]
        for u, to in ((1 - c, 2 * x + 1 - c), (2, device(far, 0)), (3, device(far, 1))):
            send(src.at[tile(j * NEAR + u * MAIN), cols], rx.at[dst, to_cols], tsend.at[step], trecv.at[step], to)

    def gather_overflow():
        for h in range(PARTS):
            cols = slice(h * COLS, (h + 1) * COLS)
            total = dot(extras[0], xz[0, :, cols])
            for j in range(1, NZ):
                total += dot(extras[j], xz[j, :, cols])
            sx[OVF:ROWS, cols] = total.astype(BF16)
        exchange(sx, rx, OVF, osend.at[0], orecv.at[0], 0, DIM)

    def experts(step):
        first, n = SLOTS[step][0] * BLK, len(SLOTS[step]) * BLK
        settle(n // BLK * (BLK - MAIN), FULL * COLS, xrecv.at[step])
        settle(n // BLK * (BLK - 2 * MAIN), DCOLS, trecv.at[step])
        if step == 4:
            settle(BLK - MAIN, DIM, orecv.at[0])
            n += BLK

        def hidden(i, carry):
            cols = pl.ds(pl.multiple_of(i * 256, 256), 256)
            rows = rx[first : first + n, :]
            gate, upward = dot(rows, wg[:, cols]), dot(rows, wu[:, cols])
            hid[0:n, cols] = (gate / (1.0 + jnp.exp(-gate)) * upward).astype(BF16)
            return carry

        def result(i, carry):
            cols = pl.ds(pl.multiple_of(i * 256, 256), 256)
            ys[first : first + n, cols] = dot(hid[0:n, :], wd[:, cols]).astype(BF16)
            return carry

        lax.fori_loop(0, HID // 256, hidden, 0)
        lax.fori_loop(0, DIM // 256, result, 0)

    def give_back(step):
        for h in RETURNED:
            for j in SLOTS[step]:
                if h < FULL:
                    exchange(ys, yr, j * BLK, ysend.at[step, h], yrecv.at[step, h], h * COLS, COLS)
                else:
                    give_back_shared(step, j, h)
            if step == 4:
                exchange(ys, yr, OVF, psend.at[h], precv.at[h], h * COLS, COLS)

    def give_back_shared(step, j, h):
        cols, to_cols = pl.ds(h * COLS, COLS), pl.ds((h - FULL) * COLS, COLS)
        yo[tile(j * NEAR + c * MAIN), to_cols] = ys[tile(j * BLK + mine), cols]
        yn[tile(j * NEAR + c * MAIN), to_cols] = ys[tile(j * BLK + hosted), cols]
        for core, own in ((c, True), (1 - c, False)):
            way = 1 - 2 * core
            trips = [
                (device(way, core), device(way, core), yo, 2 + c),
                (device(2, core), device(-way, core), yn, 2 + c),
            ]
            if not own:
                trips += [
                    (2 * x + core, 2 * x + core, yo, c),
                    (device(-way, core), 2 * x + core, yn, c),
                ]
            for home, to, dst, u in trips:
                send(
                    ys.at[tile(j * BLK + home * MAIN), cols], dst.at[tile(j * NEAR + u * MAIN), to_cols],
                    ysend.at[step, h], yrecv.at[step, h], to,
                )

    def forward(tables, k):
        for j in SLOTS[k]:
            tables[j].wait_recv()
            if j + 2 < NZ:
                tables[j + 2].start()

    def arrive(k, slots=None):
        forward(metas, k)
        for h in range(PARTS + DUAL):
            for way in (up, down):
                way[k - 1][h].wait_recv()
                if k < 4:
                    way[k][h].start()
            if h == PARTS:
                forward(metns, k)
            gather(k, h, slots)

    for h in range(PARTS):
        gather(0, h)
    dense_table.wait_recv()
    metns[1].start()
    metns[2].start()
    for i in range(DUAL):
        dense[i].wait_recv()
        up[0][PARTS + i].start()
        down[0][PARTS + i].start()
        gather(0, PARTS + i)
    arrive(1)
    for load in loads[3:]:
        load.wait()
    experts(0)
    arrive(2)
    experts(1)
    arrive(3, (5,))
    selections(6)
    arrive(4)
    gather_overflow()
    for h in range(PARTS + DUAL):
        gather(3, h, (6,))
    experts(2)
    experts(4)
    give_back(4)
    experts(3)
    for step in (3, 2, 1, 0):
        give_back(step)

    def combine(j, h):
        i = h - FULL if h < PARTS else h - PARTS
        cols, dual_cols = slice(h * COLS, (h + 1) * COLS), slice(i * COLS, (i + 1) * COLS)
        if h >= PARTS:
            return dot(cn[j], yn[j * NEAR : (j + 1) * NEAR, dual_cols])
        extra = dot(cm[j, :, BLK : 2 * BLK], yr[OVF:ROWS, cols])
        if h >= FULL:
            return extra + dot(co[j], yo[j * NEAR : (j + 1) * NEAR, dual_cols])
        return extra + dot(cm[j, :, 0:BLK], yr[j * BLK : (j + 1) * BLK, cols])

    settled = set()

    def returned(step, h):
        h = h - DUAL if h >= PARTS else h
        if (step, h) not in settled:
            settled.add((step, h))
            if step == 4:
                settle(BLK - MAIN, COLS, precv.at[h])
            settle(len(SLOTS[step]) * (BLK - MAIN if h < FULL else BLK - 2 * MAIN), COLS, yrecv.at[step, h])

    def homeward(way, m, lo, n):
        return [
            pltpu.make_async_remote_copy(
                src_ref=zs.at[way, m, pl.ds(lo, n), pl.ds(h * COLS, COLS)],
                dst_ref=zr.at[way, m, pl.ds(lo, n), pl.ds(h * COLS, COLS)],
                send_sem=rsend.at[way, m, h], recv_sem=rrecv.at[way, m, h],
                device_id=at_z(1 - 2 * way), device_id_type=MESH,
            )
            for h in range(PARTS + DUAL)
        ]

    spans = ((0, HALF), (HALF, HALF))
    home = [[homeward(way, 0, *spans[way])] + [homeward(way, m, 0, TOK) for m in (1, 2, 3)] for way in (0, 1)]
    final = [
        pltpu.make_async_remote_copy(
            src_ref=fs.at[:, pl.ds(i * COLS, COLS)], dst_ref=fr.at[:, pl.ds(i * COLS, COLS)],
            send_sem=fsend.at[i], recv_sem=frecv.at[i], device_id=in_row(host_of), device_id_type=MESH,
        )
        for i in range(DUAL)
    ]
    def combine_step(m):
        step = 4 - m
        for h in SECOND + RETURNED:
            cols = slice(h * COLS, (h + 1) * COLS)
            returned(step, h)
            if m == 0:
                part = combine(7, h).astype(BF16)
                for way in (0, 1):
                    lo, n = spans[way]
                    zs[way, 0, lo : lo + n, cols] = part[lo : lo + n]
                    home[way][0][h].start()
                continue
            for way, j in ((0, 2 * step), (1, 2 * step - 1)):
                part = combine(j, h)
                home[way][m - 1][h].wait_recv()
                if m == 1:
                    lo, n = spans[way]
                    came = zr[way, 0, lo : lo + n, cols].astype(F32)
                    zs[way, 1, lo : lo + n, cols] = (part[lo : lo + n] + came).astype(BF16)
                    lo = HALF - lo
                    zs[way, 1, lo : lo + n, cols] = part[lo : lo + n].astype(BF16)
                else:
                    came = zr[way, m - 1, :, cols].astype(F32)
                    zs[way, m, :, cols] = (part + came).astype(BF16)
                home[way][m][h].start()

    for m in range(4):
        combine_step(m)
    for h in SECOND + tuple(range(PARTS)):
        cols = slice(h * COLS, (h + 1) * COLS)
        returned(0, h)
        total = combine(0, h)
        for way in (0, 1):
            home[way][3][h].wait_recv()
            total += zr[way, 3, :, cols].astype(F32)
        if h >= PARTS:
            i = h - PARTS
            fs[:, i * COLS : (i + 1) * COLS] = total.astype(BF16)
            final[i].start()
            continue
        if h >= FULL:
            i = h - FULL
            final[i].wait_recv()
            total += fr[:, i * COLS : (i + 1) * COLS].astype(F32)
        out[:, cols] = total.astype(BF16)

    for message in up + down + home[0] + home[1] + [dense, final, metas[1:], metns[1:], [dense_table]]:
        for copy in message:
            copy.wait_send()
    for step in range(5):
        n = len(SLOTS[step])
        settle(n * (BLK - MAIN), FULL * COLS, xsend.at[step])
        settle(n * (BLK - 2 * MAIN), DCOLS, tsend.at[step])
        for h in range(PARTS):
            settle(n * (BLK - MAIN if h < FULL else BLK - 2 * MAIN), COLS, ysend.at[step, h])
    settle(BLK - MAIN, DIM, osend.at[0])
    for h in range(PARTS):
        settle(BLK - MAIN, COLS, psend.at[h])


def local(tokens, routes, combine_weights, w_gate, w_up, w_down):
    anywhere = pl.BlockSpec(memory_space=pl.ANY)
    dma = pltpu.SemaphoreType.DMA
    return pl.pallas_call(
        kernel,
        name="routed_experts",
        out_shape=jax.ShapeDtypeStruct((TOK, DIM), BF16),
        in_specs=[anywhere] * 6,
        out_specs=pl.BlockSpec(memory_space=pltpu.VMEM),
        scratch_shapes=[
            pltpu.VMEM((NZ, TOK, WIDE), BF16),
            pltpu.VMEM((ROWS, DIM), BF16),
            pltpu.VMEM((ROWS, DIM), BF16),
            pltpu.VMEM((ROWS, DIM), BF16),
            pltpu.VMEM((ROWS, DIM), BF16),
            pltpu.VMEM((NZ * NEAR, DCOLS), BF16),
            pltpu.VMEM((NZ * NEAR, DCOLS), BF16),
            pltpu.VMEM((NZ * NEAR, DCOLS), BF16),
            pltpu.VMEM((NZ * NEAR, DCOLS), BF16),
            pltpu.VMEM((2, 4, TOK, WIDE), BF16),
            pltpu.VMEM((2, 4, TOK, WIDE), BF16),
            pltpu.VMEM((TOK, DCOLS), BF16),
            pltpu.VMEM((TOK, DCOLS), BF16),
            pltpu.VMEM((DIM, HID), BF16),
            pltpu.VMEM((DIM, HID), BF16),
            pltpu.VMEM((HID, DIM), BF16),
            pltpu.VMEM((2 * BLK, HID), BF16),
            pltpu.VMEM((TOK, 8), jnp.int32),
            pltpu.VMEM((TOK, 8), BF16),
            pltpu.VMEM((128, 128), F32),
            pltpu.VMEM((NZ, 16, 128), F32),
            pltpu.VMEM((NZ, 16, 128), F32),
            pltpu.VMEM((NZ, TOK, 2 * BLK), BF16),
            pltpu.VMEM((NZ, TOK, NEAR), BF16),
            pltpu.VMEM((NZ, TOK, NEAR), BF16),
            dma((6,)),
            dma((8, PARTS + DUAL)), dma((8, PARTS + DUAL)), dma((8,)), dma((8,)), dma((8,)), dma((8,)),
            dma((DUAL,)), dma((DUAL,)),
            dma((5,)), dma((5,)), dma((5,)), dma((5,)), dma((1,)), dma((1,)),
            dma((5, PARTS)), dma((5, PARTS)), dma((PARTS,)), dma((PARTS,)),
            dma((2, 4, PARTS + DUAL)), dma((2, 4, PARTS + DUAL)), dma((DUAL,)), dma((DUAL,)),
        ],
        compiler_params=pltpu.CompilerParams(
            collective_id=0, has_side_effects=True, vmem_limit_bytes=67_043_328
        ),
    )(tokens, routes, combine_weights, w_gate, w_up, w_down)


def solution(mesh):
    in_specs = (
        P(("dp", "ep"), None), P(("dp", "ep"), None), P(("dp", "ep"), None),
        P("ep", None, None), P("ep", None, None), P("ep", None, None),
    )
    return jax.shard_map(
        local, mesh=mesh, in_specs=in_specs, out_specs=P(("dp", "ep"), None), check_vma=False
    )
```

time: 124 us -> 120 us (0.968)
  Pallas kernels: 119 us -> 115 us
    pallas_call x1, Pallas kernels: 119 us -> 115 us  [local(): pl.pallas_call(kernel, name='routed_experts', out_shape=jax.ShapeDtypeStr...]
where the time goes in v3:
time: 120 us
  Pallas kernels  115 us (96%)
  local copies, waits for them, and re-layouts  4.54 us (4%)
    pallas_call x1, Pallas kernels, local(): pl.pallas_call(kernel, name='routed_experts', out_shape=jax.ShapeDtypeStr...  115 us
    unnamed x3, local copies, waits for them, and re-layouts  4.54 us

profile of v3, /device:TPU:1, one launch (start us, length us, event | category | flops | bytes accessed | tf_op | source)
XLA Modules:
  0.0 119.8 jit_solution(8865744322602398317)
XLA Ops:
  0.0 1.4 %copy.8.weights = bf16[96,8]{1,0:T(8,128)(2,1)} copy(bf16[96,8]{0,1:T(8,128)(2,1)} %param.8) | data formatting | bytes 3072 | tf_op args[2]
  1.4 1.4 %copy.7.routes = s32[96,8]{1,0:T(8,128)} copy(s32[96,8]{0,1:T(8,128)} %param.7) | data formatting | bytes 6144 | tf_op args[1]
  2.8 115.3 %routed_experts.1 = bf16[96,2048]{1,0:T(8,128)(2,1)} custom-call(bf16[96,2048]{1,0:T(8,128)(2,1)} %tokens.1, s32[96,8]{1,0:T(8,128)} %copy.7.routes, bf16[96,8]{1,0:T(8,128)(2,1)} %copy.8.weights, bf16[1,2048,768]{2,1,0:T(8,128)(2,1)} %w_gate.1, bf16[1,2048,768]{2,1,0:T(8,128)(2,1)} %w_up.1, bf16[1,768,2048]{2,1,0:T(8,128)(2,1)} %w_down.1), custom_call_target="tpu_custom_call" | custom-call | tf_op jit(solution)/shard_map/routed_experts/pallas_call | solution.py:430
  118.1 1.8 %copy.10 = bf16[96,2048]{1,0:T(8,128)(2,1)} copy(bf16[96,2048]{1,0:T(8,128)(2,1)} %routed_experts.1) | data formatting | bytes 786432

commit v4 on v3

--- a/solution.py
+++ b/solution.py
@@ -15,6 +15,8 @@
 OVF = NZ * BLK
 ROWS = OVF + BLK
 HALF = TOK // 2
+EARLY = 2
+LIMIT = 60 * 2**20
 NEAR = 4 * MAIN
 
 PARTS, DUAL = 4, 1
@@ -39,8 +41,8 @@
 
 def kernel(
     tokens, routes, weights, w_gate, w_up, w_down, out,
-    xz, sx, rx, ys, yr, so, sn, yo, yn, zs, zr, fs, fr,
-    wg, wu, wd, hid, listed, weighed, square, meta, metn, cm, co, cn,
+    done, xz, sx, rx, ys, yr, so, sn, yo, yn, zs, zr, fs, fr,
+    wg, wu, wd, hid, listed, weighed, meta, metn, cm, co, cn,
     local_sem, zsend, zrecv, msend, mrecv, nsend, nrecv, dsend, drecv,
     xsend, xrecv, tsend, trecv, osend, orecv, ysend, yrecv, psend, precv, rsend, rrecv, fsend, frecv,
 ):
@@ -78,12 +80,11 @@
     for load in loads:
         load.start()
 
-    square[...] = jnp.full((128, 128), -1.0, F32)
+    meta[0] = jnp.full((16, 128), -1.0, F32)
     loads[0].wait()
-    square[0:TOK, 0:8] = listed[...].astype(F32)
+    meta[0, 0:8, 0:TOK] = listed[...].astype(F32)
     loads[1].wait()
-    square[0:TOK, 8:16] = weighed[...].astype(F32)
-    meta[0] = jnp.transpose(square[...])[0:16]
+    meta[0, 8:16, 0:TOK] = weighed[...].astype(F32)
 
     def ring(k, src, dst, sem, lo=0, n=TOK):
         return [
@@ -92,7 +93,7 @@
                 dst_ref=xz.at[dst, pl.ds(lo, n), pl.ds(h * COLS, COLS)],
                 send_sem=zsend.at[sem, h], recv_sem=zrecv.at[sem, h], device_id=at_z(k), device_id_type=MESH,
             )
-            for h in range(PARTS + DUAL)
+            for h in range(PARTS + DUAL if n == TOK else PARTS)
         ]
 
     def tables(ref, send, recv):
@@ -106,7 +107,7 @@
 
     up = [ring(1, 0, 1, 0), ring(1, 1, 3, 2), ring(1, 3, 5, 4), ring(1, 5, 7, 6, 0, HALF)]
     down = [ring(-1, 0, 2, 1), ring(-1, 2, 4, 3), ring(-1, 4, 6, 5), ring(-1, 6, 7, 7, HALF, HALF)]
-    metas, metns = tables(meta, msend, mrecv), tables(metn, nsend, nrecv)
+    metas, metns = tables(meta, msend, mrecv), tables(metn, nsend, nrecv)[:-1]
     dense = [
         pltpu.make_async_remote_copy(
             src_ref=xz.at[0, :, pl.ds((FULL + i) * COLS, COLS)], dst_ref=xz.at[0, :, pl.ds((PARTS + i) * COLS, COLS)],
@@ -165,7 +166,8 @@
         picks[j] = pick(place_j == (row % MAIN).astype(F32), weight_j, cm, j, 0, BLK)
         extra = (place_j == (MAIN + row % 2).astype(F32)) & (row % MAIN // 2 == j)
         extras[j] = pick(extra, weight_j, cm, j, BLK, BLK)
-        own_picks[j] = pick(dot(own_rows, place) == (near % MAIN).astype(F32), dot(own_rows, weight), co, j, 0, NEAR)
+        if j < 7:
+            own_picks[j] = pick(dot(own_rows, place) == (near % MAIN).astype(F32), dot(own_rows, weight), co, j, 0, NEAR)
 
     def second_selections(j):
         place, weight = lists(metn, j)
@@ -195,7 +197,7 @@
         for j in slots or SLOTS[step]:
             if j not in picks:
                 selections(j)
-            if h < FULL:
+            if h < FULL or (step == 4 and h < PARTS):
                 sx[j * BLK : (j + 1) * BLK, h * COLS : (h + 1) * COLS] = dot(
                     picks[j], xz[j, :, h * COLS : (h + 1) * COLS]
                 ).astype(BF16)
@@ -226,31 +228,25 @@
 
     def experts(step):
         first, n = SLOTS[step][0] * BLK, len(SLOTS[step]) * BLK
-        settle(n // BLK * (BLK - MAIN), FULL * COLS, xrecv.at[step])
-        settle(n // BLK * (BLK - 2 * MAIN), DCOLS, trecv.at[step])
         if step == 4:
+            settle(BLK - MAIN, DIM, xrecv.at[step])
             settle(BLK - MAIN, DIM, orecv.at[0])
             n += BLK
-
-        def hidden(i, carry):
-            cols = pl.ds(pl.multiple_of(i * 256, 256), 256)
+        else:
+            settle(n // BLK * (BLK - MAIN), FULL * COLS, xrecv.at[step])
+            settle(n // BLK * (BLK - 2 * MAIN), DCOLS, trecv.at[step])
+
+        for i in range(0, HID, 256):
             rows = rx[first : first + n, :]
-            gate, upward = dot(rows, wg[:, cols]), dot(rows, wu[:, cols])
-            hid[0:n, cols] = (gate / (1.0 + jnp.exp(-gate)) * upward).astype(BF16)
-            return carry
-
-        def result(i, carry):
-            cols = pl.ds(pl.multiple_of(i * 256, 256), 256)
-            ys[first : first + n, cols] = dot(hid[0:n, :], wd[:, cols]).astype(BF16)
-            return carry
-
-        lax.fori_loop(0, HID // 256, hidden, 0)
-        lax.fori_loop(0, DIM // 256, result, 0)
+            gate, upward = dot(rows, wg[:, i : i + 256]), dot(rows, wu[:, i : i + 256])
+            hid[0:n, i : i + 256] = (gate / (1.0 + jnp.exp(-gate)) * upward).astype(BF16)
+        for i in range(0, DIM, 512):
+            ys[first : first + n, i : i + 512] = dot(hid[0:n, :], wd[:, i : i + 512]).astype(BF16)
 
     def give_back(step):
         for h in RETURNED:
             for j in SLOTS[step]:
-                if h < FULL:
+                if h < FULL or step == 4:
                     exchange(ys, yr, j * BLK, ysend.at[step, h], yrecv.at[step, h], h * COLS, COLS)
                 else:
                     give_back_shared(step, j, h)
@@ -281,18 +277,25 @@
     def forward(tables, k):
         for j in SLOTS[k]:
             tables[j].wait_recv()
-            if j + 2 < NZ:
+            if j + 2 < len(tables):
                 tables[j + 2].start()
 
-    def arrive(k, slots=None):
+    def arrive(k, slots=None, early=0):
         forward(metas, k)
-        for h in range(PARTS + DUAL):
-            for way in (up, down):
-                way[k - 1][h].wait_recv()
-                if k < 4:
-                    way[k][h].start()
-            if h == PARTS:
-                forward(metns, k)
+        for h in range(PARTS):
+            pass_on(k, h)
+            gather(k, h, SLOTS[k] if h < early else slots)
+
+    def pass_on(k, h):
+        for way in (up, down):
+            way[k - 1][h].wait_recv()
+            if k < (4 if h < PARTS else 3):
+                way[k][h].start()
+
+    def arrive_second(k, slots=None):
+        forward(metns, k)
+        for h in SECOND:
+            pass_on(k, h)
             gather(k, h, slots)
 
     for h in range(PARTS):
@@ -302,21 +305,24 @@
     metns[2].start()
     for i in range(DUAL):
         dense[i].wait_recv()
-        up[0][PARTS + i].start()
-        down[0][PARTS + i].start()
         gather(0, PARTS + i)
     arrive(1)
+    for h in SECOND:
+        up[0][h].start()
+        down[0][h].start()
     for load in loads[3:]:
         load.wait()
     experts(0)
     arrive(2)
-    experts(1)
-    arrive(3, (5,))
-    selections(6)
+    arrive_second(1)
+    arrive(3, (5,), EARLY)
+    arrive_second(2)
     arrive(4)
     gather_overflow()
-    for h in range(PARTS + DUAL):
+    for h in range(EARLY, PARTS):
         gather(3, h, (6,))
+    arrive_second(3)
+    experts(1)
     experts(2)
     experts(4)
     give_back(4)
@@ -330,7 +336,7 @@
         if h >= PARTS:
             return dot(cn[j], yn[j * NEAR : (j + 1) * NEAR, dual_cols])
         extra = dot(cm[j, :, BLK : 2 * BLK], yr[OVF:ROWS, cols])
-        if h >= FULL:
+        if h >= FULL and j < 7:
             return extra + dot(co[j], yo[j * NEAR : (j + 1) * NEAR, dual_cols])
         return extra + dot(cm[j, :, 0:BLK], yr[j * BLK : (j + 1) * BLK, cols])
 
@@ -342,7 +348,7 @@
             settled.add((step, h))
             if step == 4:
                 settle(BLK - MAIN, COLS, precv.at[h])
-            settle(len(SLOTS[step]) * (BLK - MAIN if h < FULL else BLK - 2 * MAIN), COLS, yrecv.at[step, h])
+            settle(len(SLOTS[step]) * (BLK - MAIN if h < FULL or step == 4 else BLK - 2 * MAIN), COLS, yrecv.at[step, h])
 
     def homeward(way, m, lo, n):
         return [
@@ -352,7 +358,7 @@
                 send_sem=rsend.at[way, m, h], recv_sem=rrecv.at[way, m, h],
                 device_id=at_z(1 - 2 * way), device_id_type=MESH,
             )
-            for h in range(PARTS + DUAL)
+            for h in range(PARTS + DUAL if m else PARTS)
         ]
 
     spans = ((0, HALF), (HALF, HALF))
@@ -366,7 +372,7 @@
     ]
     def combine_step(m):
         step = 4 - m
-        for h in SECOND + RETURNED:
+        for h in (SECOND if m else ()) + RETURNED:
             cols = slice(h * COLS, (h + 1) * COLS)
             returned(step, h)
             if m == 0:
@@ -378,6 +384,10 @@
                 continue
             for way, j in ((0, 2 * step), (1, 2 * step - 1)):
                 part = combine(j, h)
+                if m == 1 and h >= PARTS:
+                    zs[way, 1, :, cols] = part.astype(BF16)
+                    home[way][1][h].start()
+                    continue
                 home[way][m - 1][h].wait_recv()
                 if m == 1:
                     lo, n = spans[way]
@@ -392,6 +402,7 @@
 
     for m in range(4):
         combine_step(m)
+    stores = []
     for h in SECOND + tuple(range(PARTS)):
         cols = slice(h * COLS, (h + 1) * COLS)
         returned(0, h)
@@ -408,32 +419,38 @@
             i = h - FULL
             final[i].wait_recv()
             total += fr[:, i * COLS : (i + 1) * COLS].astype(F32)
-        out[:, cols] = total.astype(BF16)
+        done[:, cols] = total.astype(BF16)
+        stores.append(pltpu.make_async_copy(done.at[:, cols], out.at[:, cols], local_sem.at[6 + h]))
+        stores[-1].start()
 
     for message in up + down + home[0] + home[1] + [dense, final, metas[1:], metns[1:], [dense_table]]:
         for copy in message:
             copy.wait_send()
     for step in range(5):
         n = len(SLOTS[step])
-        settle(n * (BLK - MAIN), FULL * COLS, xsend.at[step])
-        settle(n * (BLK - 2 * MAIN), DCOLS, tsend.at[step])
+        settle(n * (BLK - MAIN), DIM if step == 4 else FULL * COLS, xsend.at[step])
+        if step < 4:
+            settle(n * (BLK - 2 * MAIN), DCOLS, tsend.at[step])
         for h in range(PARTS):
-            settle(n * (BLK - MAIN if h < FULL else BLK - 2 * MAIN), COLS, ysend.at[step, h])
+            settle(n * (BLK - MAIN if h < FULL or step == 4 else BLK - 2 * MAIN), COLS, ysend.at[step, h])
+    for store in stores:
+        store.wait()
     settle(BLK - MAIN, DIM, osend.at[0])
     for h in range(PARTS):
         settle(BLK - MAIN, COLS, psend.at[h])
 
 
 def local(tokens, routes, combine_weights, w_gate, w_up, w_down):
-    anywhere = pl.BlockSpec(memory_space=pl.ANY)
+    in_hbm = pl.BlockSpec(memory_space=pltpu.HBM)
     dma = pltpu.SemaphoreType.DMA
     return pl.pallas_call(
         kernel,
         name="routed_experts",
         out_shape=jax.ShapeDtypeStruct((TOK, DIM), BF16),
-        in_specs=[anywhere] * 6,
-        out_specs=pl.BlockSpec(memory_space=pltpu.VMEM),
+        in_specs=[in_hbm] * 6,
+        out_specs=in_hbm,
         scratch_shapes=[
+            pltpu.VMEM((TOK, DIM), BF16),
             pltpu.VMEM((NZ, TOK, WIDE), BF16),
             pltpu.VMEM((ROWS, DIM), BF16),
             pltpu.VMEM((ROWS, DIM), BF16),
@@ -451,15 +468,14 @@
             pltpu.VMEM((DIM, HID), BF16),
             pltpu.VMEM((HID, DIM), BF16),
             pltpu.VMEM((2 * BLK, HID), BF16),
-            pltpu.VMEM((TOK, 8), jnp.int32),
-            pltpu.VMEM((TOK, 8), BF16),
-            pltpu.VMEM((128, 128), F32),
+            pltpu.VMEM((8, TOK), jnp.int32),
+            pltpu.VMEM((8, TOK), BF16),
             pltpu.VMEM((NZ, 16, 128), F32),
             pltpu.VMEM((NZ, 16, 128), F32),
             pltpu.VMEM((NZ, TOK, 2 * BLK), BF16),
             pltpu.VMEM((NZ, TOK, NEAR), BF16),
             pltpu.VMEM((NZ, TOK, NEAR), BF16),
-            dma((6,)),
+            dma((6 + PARTS,)),
             dma((8, PARTS + DUAL)), dma((8, PARTS + DUAL)), dma((8,)), dma((8,)), dma((8,)), dma((8,)),
             dma((DUAL,)), dma((DUAL,)),
             dma((5,)), dma((5,)), dma((5,)), dma((5,)), dma((1,)), dma((1,)),
@@ -467,9 +483,9 @@
             dma((2, 4, PARTS + DUAL)), dma((2, 4, PARTS + DUAL)), dma((DUAL,)), dma((DUAL,)),
         ],
         compiler_params=pltpu.CompilerParams(
-            collective_id=0, has_side_effects=True, vmem_limit_bytes=67_043_328
+            collective_id=0, has_side_effects=True, vmem_limit_bytes=LIMIT
         ),
-    )(tokens, routes, combine_weights, w_gate, w_up, w_down)
+    )(tokens, routes.T, combine_weights.T, w_gate, w_up, w_down)
 
 
 def solution(mesh):

time: 120 us -> 114 us (0.950)
  Pallas kernels: 115 us -> 112 us
  local copies, waits for them, and re-layouts: 4.54 us -> 1.77 us
    pallas_call x1, Pallas kernels: 115 us -> 112 us  [local(): pl.pallas_call(kernel, name='routed_experts', out_shape=jax.ShapeDtypeStr...]
    unnamed x3 -> x1, local copies, waits for them, and re-layouts: 4.54 us -> 1.77 us
where the time goes in v4:
time: 114 us
  Pallas kernels  112 us (98%)
  local copies, waits for them, and re-layouts  1.77 us (2%)
    pallas_call x1, Pallas kernels, local(): pl.pallas_call(kernel, name='routed_experts', out_shape=jax.ShapeDtypeStr...  112 us

profile of v4, /device:TPU:1, one launch (start us, length us, event | category | flops | bytes accessed | tf_op | source)
XLA Modules:
  0.0 114.1 jit_solution(3492350674438753177)
XLA Ops:
  0.0 112.4 %routed_experts.1 = bf16[96,2048]{1,0:T(8,128)(2,1)} custom-call(bf16[96,2048]{1,0:T(8,128)(2,1)} %tokens.1, s32[8,96]{1,0:T(8,128)} %bitcast.2, bf16[8,96]{1,0:T(8,128)(2,1)} %bitcast.3, bf16[1,2048,768]{2,1,0:T(8,128)(2,1)} %w_gate.1, bf16[1,2048,768]{2,1,0:T(8,128)(2,1)} %w_up.1, bf16[1,768,2048]{2,1,0:T(8,128)(2,1)} %w_down.1), custom_call_target="tpu_custom_call" | custom-call | tf_op jit(solution)/shard_map/routed_experts/pallas_call | solution.py:446
  112.4 1.8 %copy.8 = bf16[96,2048]{1,0:T(8,128)(2,1)} copy(bf16[96,2048]{1,0:T(8,128)(2,1)} %routed_experts.1) | data formatting | bytes 786432

commit v5 on v4

--- a/solution.py
+++ b/solution.py
@@ -16,7 +16,7 @@
 ROWS = OVF + BLK
 HALF = TOK // 2
 EARLY = 2
-LIMIT = 60 * 2**20
+LIMIT = 50 * 2**20
 NEAR = 4 * MAIN
 
 PARTS, DUAL = 4, 1
@@ -41,7 +41,7 @@
 
 def kernel(
     tokens, routes, weights, w_gate, w_up, w_down, out,
-    done, xz, sx, rx, ys, yr, so, sn, yo, yn, zs, zr, fs, fr,
+    xz, sx, rx, ys, yr, so, sn, yo, yn, zs, zr, fs, fr,
     wg, wu, wd, hid, listed, weighed, meta, metn, cm, co, cn,
     local_sem, zsend, zrecv, msend, mrecv, nsend, nrecv, dsend, drecv,
     xsend, xrecv, tsend, trecv, osend, orecv, ysend, yrecv, psend, precv, rsend, rrecv, fsend, frecv,
@@ -226,7 +226,7 @@
             sx[OVF:ROWS, cols] = total.astype(BF16)
         exchange(sx, rx, OVF, osend.at[0], orecv.at[0], 0, DIM)
 
-    def experts(step):
+    def experts(step, then=None):
         first, n = SLOTS[step][0] * BLK, len(SLOTS[step]) * BLK
         if step == 4:
             settle(BLK - MAIN, DIM, xrecv.at[step])
@@ -240,18 +240,20 @@
             rows = rx[first : first + n, :]
             gate, upward = dot(rows, wg[:, i : i + 256]), dot(rows, wu[:, i : i + 256])
             hid[0:n, i : i + 256] = (gate / (1.0 + jnp.exp(-gate)) * upward).astype(BF16)
-        for i in range(0, DIM, 512):
-            ys[first : first + n, i : i + 512] = dot(hid[0:n, :], wd[:, i : i + 512]).astype(BF16)
-
-    def give_back(step):
         for h in RETURNED:
-            for j in SLOTS[step]:
-                if h < FULL or step == 4:
-                    exchange(ys, yr, j * BLK, ysend.at[step, h], yrecv.at[step, h], h * COLS, COLS)
-                else:
-                    give_back_shared(step, j, h)
-            if step == 4:
-                exchange(ys, yr, OVF, psend.at[h], precv.at[h], h * COLS, COLS)
+            cols = slice(h * COLS, (h + 1) * COLS)
+            ys[first : first + n, cols] = dot(hid[0:n, :], wd[:, cols]).astype(BF16)
+            if then:
+                then(step, h)
+
+    def give_back(step, h):
+        for j in SLOTS[step]:
+            if h < FULL or step == 4:
+                exchange(ys, yr, j * BLK, ysend.at[step, h], yrecv.at[step, h], h * COLS, COLS)
+            else:
+                give_back_shared(step, j, h)
+        if step == 4:
+            exchange(ys, yr, OVF, psend.at[h], precv.at[h], h * COLS, COLS)
 
     def give_back_shared(step, j, h):
         cols, to_cols = pl.ds(h * COLS, COLS), pl.ds((h - FULL) * COLS, COLS)
@@ -324,11 +326,11 @@
     arrive_second(3)
     experts(1)
     experts(2)
-    experts(4)
-    give_back(4)
-    experts(3)
-    for step in (3, 2, 1, 0):
-        give_back(step)
+    experts(4, give_back)
+    experts(3, give_back)
+    for step in (2, 1, 0):
+        for h in RETURNED:
+            give_back(step, h)
 
     def combine(j, h):
         i = h - FULL if h < PARTS else h - PARTS
@@ -402,7 +404,6 @@
 
     for m in range(4):
         combine_step(m)
-    stores = []
     for h in SECOND + tuple(range(PARTS)):
         cols = slice(h * COLS, (h + 1) * COLS)
         returned(0, h)
@@ -419,9 +420,7 @@
             i = h - FULL
             final[i].wait_recv()
             total += fr[:, i * COLS : (i + 1) * COLS].astype(F32)
-        done[:, cols] = total.astype(BF16)
-        stores.append(pltpu.make_async_copy(done.at[:, cols], out.at[:, cols], local_sem.at[6 + h]))
-        stores[-1].start()
+        out[:, cols] = total.astype(BF16)
 
     for message in up + down + home[0] + home[1] + [dense, final, metas[1:], metns[1:], [dense_table]]:
         for copy in message:
@@ -433,11 +432,13 @@
             settle(n * (BLK - 2 * MAIN), DCOLS, tsend.at[step])
         for h in range(PARTS):
             settle(n * (BLK - MAIN if h < FULL or step == 4 else BLK - 2 * MAIN), COLS, ysend.at[step, h])
-    for store in stores:
-        store.wait()
     settle(BLK - MAIN, DIM, osend.at[0])
     for h in range(PARTS):
         settle(BLK - MAIN, COLS, psend.at[h])
+
+
+def hold(a):
+    return pltpu.with_memory_space_constraint(a, pltpu.HBM)
 
 
 def local(tokens, routes, combine_weights, w_gate, w_up, w_down):
@@ -448,9 +449,8 @@
         name="routed_experts",
         out_shape=jax.ShapeDtypeStruct((TOK, DIM), BF16),
         in_specs=[in_hbm] * 6,
-        out_specs=in_hbm,
+        out_specs=pl.BlockSpec(memory_space=pltpu.VMEM),
         scratch_shapes=[
-            pltpu.VMEM((TOK, DIM), BF16),
             pltpu.VMEM((NZ, TOK, WIDE), BF16),
             pltpu.VMEM((ROWS, DIM), BF16),
             pltpu.VMEM((ROWS, DIM), BF16),
@@ -475,7 +475,7 @@
             pltpu.VMEM((NZ, TOK, 2 * BLK), BF16),
             pltpu.VMEM((NZ, TOK, NEAR), BF16),
             pltpu.VMEM((NZ, TOK, NEAR), BF16),
-            dma((6 + PARTS,)),
+            dma((6,)),
             dma((8, PARTS + DUAL)), dma((8, PARTS + DUAL)), dma((8,)), dma((8,)), dma((8,)), dma((8,)),
             dma((DUAL,)), dma((DUAL,)),
             dma((5,)), dma((5,)), dma((5,)), dma((5,)), dma((1,)), dma((1,)),
@@ -485,7 +485,7 @@
         compiler_params=pltpu.CompilerParams(
             collective_id=0, has_side_effects=True, vmem_limit_bytes=LIMIT
         ),
-    )(tokens, routes.T, combine_weights.T, w_gate, w_up, w_down)
+    )(*(hold(a) for a in (tokens, routes.T, combine_weights.T, w_gate, w_up, w_down)))
 
 
 def solution(mesh):

time: 114 us -> 112 us (0.982)
  no operation moved by 1% of the time
where the time goes in v5:
time: 112 us
  Pallas kernels  111 us (99%)
    pallas_call x1, Pallas kernels, local(): pl.pallas_call(kernel, name='routed_experts', out_shape=jax.ShapeDtypeStr...  111 us

profile of v5, /device:TPU:1, one launch (start us, length us, event | category | flops | bytes accessed | tf_op | source)
XLA Modules:
  0.0 112.0 jit_solution(13266612263038307339)
XLA Ops:
  0.0 111.2 %routed_experts.1 = bf16[96,2048]{1,0:T(8,128)(2,1)S(1)} custom-call(bf16[96,2048]{1,0:T(8,128)(2,1)} %tokens.1, s32[8,96]{1,0:T(8,128)} %bitcast.2, bf16[8,96]{1,0:T(8,128)(2,1)} %bitcast.3, bf16[1,2048,768]{2,1,0:T(8,128)(2,1)} %w_gate.1, bf16[1,2048,768]{2,1,0:T(8,128)(2,1)} %w_up.1, bf16[1,768,2048]{2,1,0:T(8,128)(2,1)} %w_down.1), custom_call_target="tpu_custom_call" | custom-call | tf_op jit(solution)/shard_map/routed_experts/pallas_call | solution.py:447
  111.3 0.7 copy.8

commit v6 on v5

--- a/solution.py
+++ b/solution.py
@@ -248,7 +248,7 @@
 
     def give_back(step, h):
         for j in SLOTS[step]:
-            if h < FULL or step == 4:
+            if h < FULL or step > 2:
                 exchange(ys, yr, j * BLK, ysend.at[step, h], yrecv.at[step, h], h * COLS, COLS)
             else:
                 give_back_shared(step, j, h)
@@ -326,10 +326,13 @@
     arrive_second(3)
     experts(1)
     experts(2)
+    for step in (2, 1, 0):
+        for h in range(FULL, PARTS):
+            give_back(step, h)
     experts(4, give_back)
     experts(3, give_back)
     for step in (2, 1, 0):
-        for h in RETURNED:
+        for h in range(FULL):
             give_back(step, h)
 
     def combine(j, h):
@@ -338,7 +341,7 @@
         if h >= PARTS:
             return dot(cn[j], yn[j * NEAR : (j + 1) * NEAR, dual_cols])
         extra = dot(cm[j, :, BLK : 2 * BLK], yr[OVF:ROWS, cols])
-        if h >= FULL and j < 7:
+        if h >= FULL and j < 5:
             return extra + dot(co[j], yo[j * NEAR : (j + 1) * NEAR, dual_cols])
         return extra + dot(cm[j, :, 0:BLK], yr[j * BLK : (j + 1) * BLK, cols])
 
@@ -350,7 +353,7 @@
             settled.add((step, h))
             if step == 4:
                 settle(BLK - MAIN, COLS, precv.at[h])
-            settle(len(SLOTS[step]) * (BLK - MAIN if h < FULL or step == 4 else BLK - 2 * MAIN), COLS, yrecv.at[step, h])
+            settle(len(SLOTS[step]) * (BLK - MAIN if h < FULL or step > 2 else BLK - 2 * MAIN), COLS, yrecv.at[step, h])
 
     def homeward(way, m, lo, n):
         return [
@@ -360,7 +363,7 @@
                 send_sem=rsend.at[way, m, h], recv_sem=rrecv.at[way, m, h],
                 device_id=at_z(1 - 2 * way), device_id_type=MESH,
             )
-            for h in range(PARTS + DUAL if m else PARTS)
+            for h in range(PARTS + DUAL if m > 1 else PARTS)
         ]
 
     spans = ((0, HALF), (HALF, HALF))
@@ -374,7 +377,7 @@
     ]
     def combine_step(m):
         step = 4 - m
-        for h in (SECOND if m else ()) + RETURNED:
+        for h in RETURNED:
             cols = slice(h * COLS, (h + 1) * COLS)
             returned(step, h)
             if m == 0:
@@ -386,10 +389,6 @@
                 continue
             for way, j in ((0, 2 * step), (1, 2 * step - 1)):
                 part = combine(j, h)
-                if m == 1 and h >= PARTS:
-                    zs[way, 1, :, cols] = part.astype(BF16)
-                    home[way][1][h].start()
-                    continue
                 home[way][m - 1][h].wait_recv()
                 if m == 1:
                     lo, n = spans[way]
@@ -402,20 +401,39 @@
                     zs[way, m, :, cols] = (part + came).astype(BF16)
                 home[way][m][h].start()
 
+    def second_step(m):
+        step = 4 - m
+        for h in SECOND:
+            i = h - PARTS
+            cols = slice(h * COLS, (h + 1) * COLS)
+            returned(step, h)
+            if m == 4:
+                total = combine(0, h)
+                for way in (0, 1):
+                    home[way][3][h].wait_recv()
+                    total += zr[way, 3, :, cols].astype(F32)
+                fs[:, i * COLS : (i + 1) * COLS] = total.astype(BF16)
+                final[i].start()
+                continue
+            for way, j in ((0, 2 * step), (1, 2 * step - 1)):
+                part = combine(j, h)
+                if m == 3:
+                    home[way][2][h].wait_recv()
+                    part += zr[way, 2, :, cols].astype(F32)
+                zs[way, m, :, cols] = part.astype(BF16)
+                home[way][m][h].start()
+
     for m in range(4):
+        if m < 3:
+            second_step(m + 2)
         combine_step(m)
-    for h in SECOND + tuple(range(PARTS)):
+    for h in range(PARTS):
         cols = slice(h * COLS, (h + 1) * COLS)
         returned(0, h)
         total = combine(0, h)
         for way in (0, 1):
             home[way][3][h].wait_recv()
             total += zr[way, 3, :, cols].astype(F32)
-        if h >= PARTS:
-            i = h - PARTS
-            fs[:, i * COLS : (i + 1) * COLS] = total.astype(BF16)
-            final[i].start()
-            continue
         if h >= FULL:
             i = h - FULL
             final[i].wait_recv()
@@ -431,7 +449,7 @@
         if step < 4:
             settle(n * (BLK - 2 * MAIN), DCOLS, tsend.at[step])
         for h in range(PARTS):
-            settle(n * (BLK - MAIN if h < FULL or step == 4 else BLK - 2 * MAIN), COLS, ysend.at[step, h])
+            settle(n * (BLK - MAIN if h < FULL or step > 2 else BLK - 2 * MAIN), COLS, ysend.at[step, h])
     settle(BLK - MAIN, DIM, osend.at[0])
     for h in range(PARTS):
         settle(BLK - MAIN, COLS, psend.at[h])

time: 112 us -> 111 us (level)
    pallas_call x1, Pallas kernels: 111 us -> 110 us  [local(): pl.pallas_call(kernel, name='routed_experts', out_shape=jax.ShapeDtypeStr...]
where the time goes in v6:
time: 111 us
  Pallas kernels  110 us (99%)
    pallas_call x1, Pallas kernels, local(): pl.pallas_call(kernel, name='routed_experts', out_shape=jax.ShapeDtypeStr...  110 us

profile of v6, /device:TPU:1, one launch (start us, length us, event | category | flops | bytes accessed | tf_op | source)
XLA Modules:
  0.0 110.7 jit_solution(2090083974061411594)
XLA Ops:
  0.0 110.0 %routed_experts.1 = bf16[96,2048]{1,0:T(8,128)(2,1)S(1)} custom-call(bf16[96,2048]{1,0:T(8,128)(2,1)} %tokens.1, s32[8,96]{1,0:T(8,128)} %bitcast.2, bf16[8,96]{1,0:T(8,128)(2,1)} %bitcast.3, bf16[1,2048,768]{2,1,0:T(8,128)(2,1)} %w_gate.1, bf16[1,2048,768]{2,1,0:T(8,128)(2,1)} %w_up.1, bf16[1,768,2048]{2,1,0:T(8,128)(2,1)} %w_down.1), custom_call_target="tpu_custom_call" | custom-call | tf_op jit(solution)/shard_map/routed_experts/pallas_call | solution.py:465
  110.0 0.7 copy.8
